TPU v7x, 256 devices: a whole 4x4x8 slice. The times are simulated.
256 devices in a mesh: col: 32 (over z, y), row: 8 (over x, core).
Axes of the slice: x: 4, y: 4, z: 8, core: 2. Of those that a mesh axis runs over, the one named last changes fastest.
Arguments:
- psi_start: float32 [2048, 3, 3, 2048], P('row', None, None, 'col')
- left_env: float32 [2048, 5, 2048], P('row')
- right_env: float32 [2048, 5, 2048], P('col')
- mpo_pair: float32 [5, 5, 3, 3, 3, 3], replicated
Outputs:
- output 1: float32 [4], replicated
- output 2: float32 [4], replicated
- output 3: float32 [2048, 3, 3, 2048], P('row', None, None, 'col')
All inputs are finite; a program needn't handle non-finite values.
Results may differ from a plain program's by a relative error of at most 0.001.
Values sent between devices are 32-bit elements.
A program may use at most 768 MiB of HBM per device.

v0:
```python
import jax
import jax.numpy as jnp
from jax import lax
from jax.sharding import PartitionSpec as P

LANCZOS_STEPS = 4
FULL_PREC = lax.Precision.HIGHEST


def solution(mesh):
    row_size = mesh.shape['row']
    col_size = mesh.shape['col']

    def local_run(psi_blk, left_blk, right_blk, mpo_pair):
        num_elems = float(psi_blk.size * row_size * col_size)
        left_cols = lax.all_to_all(left_blk, 'row', 2, 0, tiled=True)

        def mean_dot(left_vec, right_vec):
            return lax.psum(jnp.sum(left_vec * right_vec), ('col', 'row')) / num_elems

        def apply_ham(vec_blk):
            gathered = lax.all_gather(vec_blk, 'row', axis=0, tiled=True)
            stage_one = jnp.einsum('alc,asub->lcsub', left_cols, gathered, precision=FULL_PREC, preferred_element_type=jnp.float32)
            stage_two = jnp.einsum('lrsutq,lcsub->rctqb', mpo_pair, stage_one, precision=FULL_PREC, preferred_element_type=jnp.float32)
            part_out = jnp.einsum('rctqb,bre->ctqe', stage_two, right_blk, precision=FULL_PREC, preferred_element_type=jnp.float32)
            return lax.psum_scatter(part_out, 'col', scatter_dimension=3, tiled=True)

        cur_vec = psi_blk * lax.rsqrt(mean_dot(psi_blk, psi_blk))
        prev_vec = cur_vec
        alpha_list = []
        beta_list = []
        for step_idx in range(LANCZOS_STEPS):
            h_vec = apply_ham(cur_vec)
            alpha_j = mean_dot(cur_vec, h_vec)
            residual = h_vec - alpha_j * cur_vec
            if step_idx > 0:
                residual = residual - beta_list[-1] * prev_vec
            beta_j = jnp.sqrt(mean_dot(residual, residual))
            alpha_list.append(alpha_j)
            beta_list.append(beta_j)
            prev_vec = cur_vec
            cur_vec = residual / beta_j
        return jnp.stack(alpha_list), jnp.stack(beta_list), cur_vec

    return jax.shard_map(local_run, mesh=mesh, in_specs=(P('row', None, None, 'col'), P('row', None, None), P('col', None, None), P()), out_specs=(P(), P(), P('row', None, None, 'col')), check_vma=False)
```

profile of v0, /device:TPU:1, one launch (start us, length us, event | category | flops | bytes accessed | tf_op | source)
XLA Modules:
  0.0 2328.6 jit_solution(10494066703506007026)
XLA Ops:
  7.2 15.4 copy.21
  22.6 8.9 all-to-all-start
  31.6 0.8 multiply_reduce_fusion.8
  32.3 251.3 %psum.63 = f32[]{:T(128)} all-reduce(f32[]{:T(128)} %multiply_reduce_fusion.8), channel_id=1, replica_groups=mesh['col'=32,'row'=8] {'col','row'}, use_global_device_ids=true, to_apply=%region_1.0 | all-reduce | flops 1 | bytes 8 | tf_op jit(solution)/shard_map/psum | solution.py:19
  284.3 0.9 broadcast_multiply_fusion
  285.2 1.6 copy.25
  286.8 15.3 copy.23
  302.1 15.8 all-gather.5.cloned.1.call-done
  317.9 22.8 fusion.36
  340.7 8.0 fusion.24
  348.7 34.4 %convolution_bitcast_fusion.3 = f32[256,3,3,2048]{0,3,2,1:T(8,128)} fusion(f32[5,256,3,3,64]{1,0,3,2,4:T(8,128)S(1)} %fusion.24, f32[64,5,2048]{2,0,1:T(8,128)S(1)} %copy-done), kind=kOutput, calls=%fused_computation.3 | convolution fusion | flops 18119393280 | bytes 24444928 | tf_op jit(solution)/shard_map/rctqb,bre->ctqe/dot_general | solution.py:25
  383.2 247.5 %reduce-scatter.5.cloned.1.call-done = f32[256,3,3,64]{0,3,2,1:T(8,128)} async-done(((f32[256,3,3,2048]{0,3,2,1:T(8,128)}), f32[256,3,3,64]{0,3,2,1:T(8,128)}) %reduce-scatter.5.cloned.1.call-update) | async-done | bytes 589840 | tf_op jit(solution)/shard_map/reduce_scatter | solution.py:26
  630.7 1.8 multiply_reduce_fusion.7
  632.5 89.0 %psum.64 = f32[]{:T(128)} all-reduce(f32[]{:T(128)} %multiply_reduce_fusion.7), channel_id=1, replica_groups=mesh['col'=32,'row'=8] {'col','row'}, use_global_device_ids=true, to_apply=%region_4.0 | all-reduce | flops 1 | bytes 8 | tf_op jit(solution)/shard_map/psum | solution.py:19
  722.2 1.8 multiply_reduce_fusion.6
  724.0 73.2 %psum.65 = f32[]{:T(128)} all-reduce(f32[]{:T(128)} %multiply_reduce_fusion.6), channel_id=1, replica_groups=mesh['col'=32,'row'=8] {'col','row'}, use_global_device_ids=true, to_apply=%region_6.0 | all-reduce | flops 1 | bytes 8 | tf_op jit(solution)/shard_map/psum | solution.py:19
  797.9 2.0 broadcast_divide_fusion.3
  799.9 33.3 %all-gather.7.cloned.1.call-done = f32[2048,3,3,64]{0,3,2,1:T(8,128)} async-done(((f32[256,3,3,64]{0,3,2,1:T(8,128)}), f32[2048,3,3,64]{0,3,2,1:T(8,128)}) %all-gather.7.cloned.1.call-update) | async-done | bytes 4718608 | tf_op jit(solution)/shard_map/all_gather | solution.py:22
  833.2 22.8 fusion.39
  856.0 7.8 fusion.27
  863.8 34.8 %convolution_bitcast_fusion.2 = f32[256,3,3,2048]{0,3,2,1:T(8,128)} fusion(f32[5,256,3,3,64]{1,0,3,2,4:T(8,128)S(1)} %fusion.27, f32[64,5,2048]{2,0,1:T(8,128)S(1)} %copy-done), kind=kOutput, calls=%fused_computation.2 | convolution fusion | flops 18119393280 | bytes 24444928 | tf_op jit(solution)/shard_map/rctqb,bre->ctqe/dot_general | solution.py:25
  898.6 248.2 %reduce-scatter.7.cloned.1.call-done = f32[256,3,3,64]{0,3,2,1:T(8,128)} async-done(((f32[256,3,3,2048]{0,3,2,1:T(8,128)}), f32[256,3,3,64]{0,3,2,1:T(8,128)}) %reduce-scatter.7.cloned.1.call-update) | async-done | bytes 589840 | tf_op jit(solution)/shard_map/reduce_scatter | solution.py:26
  1146.8 2.0 multiply_reduce_fusion.5
  1148.8 78.9 %psum.66 = f32[]{:T(128)} all-reduce(f32[]{:T(128)} %multiply_reduce_fusion.5), channel_id=1, replica_groups=mesh['col'=32,'row'=8] {'col','row'}, use_global_device_ids=true, to_apply=%region_9.0 | all-reduce | flops 1 | bytes 8 | tf_op jit(solution)/shard_map/psum | solution.py:19
  1228.4 2.8 multiply_reduce_fusion.4
  1231.2 73.1 %psum.67 = f32[]{:T(128)} all-reduce(f32[]{:T(128)} %get-tuple-element.7), channel_id=1, replica_groups=mesh['col'=32,'row'=8] {'col','row'}, use_global_device_ids=true, to_apply=%region_11.0 | all-reduce | flops 1 | bytes 8 | tf_op jit(solution)/shard_map/psum | solution.py:19
  1305.0 2.0 broadcast_divide_fusion.2
  1307.0 33.2 %all-gather.9.cloned.1.call-done = f32[2048,3,3,64]{0,3,2,1:T(8,128)} async-done(((f32[256,3,3,64]{0,3,2,1:T(8,128)}), f32[2048,3,3,64]{0,3,2,1:T(8,128)}) %all-gather.9.cloned.1.call-update) | async-done | bytes 4718608 | tf_op jit(solution)/shard_map/all_gather | solution.py:22
  1340.2 22.8 fusion.42
  1363.0 7.8 fusion.30
  1370.8 34.8 %convolution_bitcast_fusion.1 = f32[256,3,3,2048]{0,3,2,1:T(8,128)} fusion(f32[5,256,3,3,64]{1,0,3,2,4:T(8,128)S(1)} %fusion.30, f32[64,5,2048]{2,0,1:T(8,128)S(1)} %copy-done), kind=kOutput, calls=%fused_computation.1 | convolution fusion | flops 18119393280 | bytes 24444928 | tf_op jit(solution)/shard_map/rctqb,bre->ctqe/dot_general | solution.py:25
  1405.6 248.3 %reduce-scatter.9.cloned.1.call-done = f32[256,3,3,64]{0,3,2,1:T(8,128)} async-done(((f32[256,3,3,2048]{0,3,2,1:T(8,128)}), f32[256,3,3,64]{0,3,2,1:T(8,128)}) %reduce-scatter.9.cloned.1.call-update) | async-done | bytes 589840 | tf_op jit(solution)/shard_map/reduce_scatter | solution.py:26
  1653.9 2.0 multiply_reduce_fusion.3
  1655.9 78.6 %psum.68 = f32[]{:T(128)} all-reduce(f32[]{:T(128)} %multiply_reduce_fusion.3), channel_id=1, replica_groups=mesh['col'=32,'row'=8] {'col','row'}, use_global_device_ids=true, to_apply=%region_14.0 | all-reduce | flops 1 | bytes 8 | tf_op jit(solution)/shard_map/psum | solution.py:19
  1735.2 2.8 multiply_reduce_fusion.2
  1738.0 73.2 %psum.69 = f32[]{:T(128)} all-reduce(f32[]{:T(128)} %get-tuple-element.5), channel_id=1, replica_groups=mesh['col'=32,'row'=8] {'col','row'}, use_global_device_ids=true, to_apply=%region_16.0 | all-reduce | flops 1 | bytes 8 | tf_op jit(solution)/shard_map/psum | solution.py:19
  1811.8 2.0 broadcast_divide_fusion.1
  1813.9 33.1 %all-gather.11.cloned.1.call-done = f32[2048,3,3,64]{0,3,2,1:T(8,128)} async-done(((f32[256,3,3,64]{0,3,2,1:T(8,128)}), f32[2048,3,3,64]{0,3,2,1:T(8,128)}) %all-gather.11.cloned.1.call-update) | async-done | bytes 4718608 | tf_op jit(solution)/shard_map/all_gather | solution.py:22
  1847.0 22.8 fusion.45
  1869.8 7.8 fusion.33
  1877.6 34.6 %convolution_bitcast_fusion = f32[256,3,3,2048]{0,3,2,1:T(8,128)} fusion(f32[5,256,3,3,64]{1,0,3,2,4:T(8,128)S(1)} %fusion.33, f32[64,5,2048]{2,0,1:T(8,128)S(1)} %copy-done), kind=kOutput, calls=%fused_computation | convolution fusion | flops 18119393280 | bytes 24444928 | tf_op jit(solution)/shard_map/rctqb,bre->ctqe/dot_general | solution.py:25
  1912.2 248.2 %reduce-scatter.11.cloned.1.call-done = f32[256,3,3,64]{0,3,2,1:T(8,128)} async-done(((f32[256,3,3,2048]{0,3,2,1:T(8,128)}), f32[256,3,3,64]{0,3,2,1:T(8,128)}) %reduce-scatter.11.cloned.1.call-update) | async-done | bytes 589840 | tf_op jit(solution)/shard_map/reduce_scatter | solution.py:26
  2160.4 2.0 multiply_reduce_fusion.1
  2162.4 78.5 %psum.70 = f32[]{:T(128)} all-reduce(f32[]{:T(128)} %multiply_reduce_fusion.1), channel_id=1, replica_groups=mesh['col'=32,'row'=8] {'col','row'}, use_global_device_ids=true, to_apply=%region_19.0 | all-reduce | flops 1 | bytes 8 | tf_op jit(solution)/shard_map/psum | solution.py:19
  2241.6 2.8 multiply_reduce_fusion
  2244.4 73.1 %psum.71 = f32[]{:T(128)} all-reduce(f32[]{:T(128)} %get-tuple-element.3), channel_id=1, replica_groups=mesh['col'=32,'row'=8] {'col','row'}, use_global_device_ids=true, to_apply=%region_21.0 | all-reduce | flops 1 | bytes 8 | tf_op jit(solution)/shard_map/psum | solution.py:19
  2318.2 1.9 broadcast_divide_fusion
  2320.2 0.6 pad_maximum_fusion
  (26 shorter events, 1.0 us)
Async XLA Ops:
  7.2 341.6 %copy-start = (f32[64,5,2048]{2,0,1:T(8,128)S(1)}, f32[64,5,2048]{2,0,1:T(8,128)}, u32[]{:S(2)}) copy-start(f32[64,5,2048]{2,0,1:T(8,128)} %param.6) | copy-start | bytes 7864324
  22.6 8.9 copy-start.1
  22.6 264.2 %all-to-all-start = ((f32[256,5,2048]{0,1,2:T(8,128)}), f32[256,5,2048]{0,1,2:T(8,128)}, u32[]{:S(2)}, u32[]{:S(2)}) async-start(f32[256,5,2048]{0,1,2:T(8,128)} %copy.21), calls=%async_computation | async-start | bytes 33554432 | tf_op jit(solution)/shard_map/all_to_all | solution.py:16
  31.6 286.4 %all-gather.5.cloned.1.call-start = ((), (), s32[]{:S(2)}) async-start(), calls=%async_computation.5 | async-start | bytes 5308416 | tf_op jit(solution)/shard_map/all_gather | solution.py:22
  285.2 345.5 %reduce-scatter.5.cloned.1.call-start = ((), (), s32[]{:S(2)}) async-start(), calls=%async_computation.6 | async-start | bytes 19464192 | tf_op jit(solution)/shard_map/reduce_scatter | solution.py:26
  383.2 450.1 %all-gather.7.cloned.1.call-start = ((), (), s32[]{:S(2)}) async-start(), calls=%async_computation.7 | async-start | bytes 5308416 | tf_op jit(solution)/shard_map/all_gather | solution.py:22
  799.9 347.0 %reduce-scatter.7.cloned.1.call-start = ((), (), s32[]{:S(2)}) async-start(), calls=%async_computation.8 | async-start | bytes 19464192 | tf_op jit(solution)/shard_map/reduce_scatter | solution.py:26
  898.6 441.6 %all-gather.9.cloned.1.call-start = ((), (), s32[]{:S(2)}) async-start(), calls=%async_computation.9 | async-start | bytes 5308416 | tf_op jit(solution)/shard_map/all_gather | solution.py:22
  1307.0 347.0 %reduce-scatter.9.cloned.1.call-start = ((), (), s32[]{:S(2)}) async-start(), calls=%async_computation.10 | async-start | bytes 19464192 | tf_op jit(solution)/shard_map/reduce_scatter | solution.py:26
  1405.6 329.6 %copy-start.2 = (f32[256,3,3,64]{0,3,2,1:T(8,128)S(1)}, f32[256,3,3,64]{0,3,2,1:T(8,128)}, u32[]{:S(2)}) copy-start(f32[256,3,3,64]{0,3,2,1:T(8,128)} %broadcast_divide_fusion.3) | copy-start | bytes 1769476
  1405.6 441.4 %all-gather.11.cloned.1.call-start = ((), (), s32[]{:S(2)}) async-start(), calls=%async_computation.11 | async-start | bytes 5308416 | tf_op jit(solution)/shard_map/all_gather | solution.py:22
  1813.8 346.6 %reduce-scatter.11.cloned.1.call-start = ((), (), s32[]{:S(2)}) async-start(), calls=%async_computation.12 | async-start | bytes 19464192 | tf_op jit(solution)/shard_map/reduce_scatter | solution.py:26
  1912.2 329.4 %copy-start.3 = (f32[256,3,3,64]{0,3,2,1:T(8,128)S(1)}, f32[256,3,3,64]{0,3,2,1:T(8,128)}, u32[]{:S(2)}) copy-start(f32[256,3,3,64]{0,3,2,1:T(8,128)} %get-tuple-element.8) | copy-start | bytes 1769476
Sparse Core Ops, SparseCore 0:
  285.3 32.5 all-gather.4
  383.3 247.3 reduce-scatter.4
  800.0 33.1 all-gather.6
  898.7 248.0 reduce-scatter.6
  1307.1 33.1 all-gather.8
  1405.7 248.1 reduce-scatter.8
  1814.0 33.0 all-gather.10
  1912.3 248.0 reduce-scatter.10
where the time goes:
time: 2340 us; the launch traced here: 2330 us
  waiting for transfers between devices  1110 us (47%)
  blocking collectives  869 us (37%)
  matrix products  261 us (11%)
  local copies, waits for them, and re-layouts  32.3 us (1%)
  other arithmetic  28.7 us (1%)
    reduce_scatter x4, waiting for transfers between devices, apply_ham(): return lax.psum_scatter(part_out, 'col', scatter_dimension=3, tiled=True)  992 us
    psum x9, blocking collectives, mean_dot(): return lax.psum(jnp.sum(left_vec * right_vec), ('col', 'row')) / num_elems  869 us
    dot_general x4, matrix products, apply_ham(): jnp.einsum('rctqb,bre->ctqe', stage_two, right_blk, precision=FULL_PREC,...  139 us
    all_gather x4, waiting for transfers between devices, apply_ham(): gathered = lax.all_gather(vec_blk, 'row', axis=0, tiled=True)  116 us
    dot_general x4, matrix products, apply_ham(): jnp.einsum('alc,asub->lcsub', left_cols, gathered, precision=FULL_PREC, p...  91 us
  transfers between devices with their start and end apart: 9, of which 8 were waited for; matrix products, arithmetic and copies ran while one was open for 1% of the time, Pallas kernels for 0%

commit v1 on v0

v1 whole, which is shorter than its diff:
```python
import functools

import jax
import jax.numpy as jnp
from jax import lax
from jax.experimental import pallas as pl
from jax.experimental.pallas import tpu as pltpu
from jax.sharding import Mesh, PartitionSpec as P

LANCZOS_STEPS = 4
FULL_PREC = lax.Precision.HIGHEST
MESH_IDS = pl.DeviceIdType.MESH


def fine_mesh(mesh):
    col_size, row_size = mesh.shape['col'], mesh.shape['row']
    y_size, core_size = 4, 2
    shape = (col_size // y_size, y_size, row_size // core_size, core_size)
    return Mesh(mesh.devices.reshape(shape), ('z', 'y', 'x', 'k'))


def sum_kernel(sizes, val_ref, out_ref, held, slots, send_sem, recv_sem):
    n_z, n_y, n_x, n_k = sizes
    y, z = lax.axis_index('y'), lax.axis_index('z')
    xk = lax.axis_index('x') * n_k + lax.axis_index('k')

    phases = (
        (n_y, y, lambda i: {'y': i}),
        (n_x * n_k, xk, lambda i: {'x': i // n_k, 'k': lax.rem(i, n_k)}),
        (n_z, z, lambda i: {'z': i}),
    )
    barrier = pltpu.get_barrier_semaphore()
    total = 0
    for count, me, device in phases:
        for d in range(1, count):
            pl.semaphore_signal(barrier, inc=1, device_id=device(lax.rem(me + d, count)), device_id_type=MESH_IDS)
            total += 1
    pl.semaphore_wait(barrier, total)

    value = val_ref[...]
    base = 0
    for count, me, device in phases:
        held[base] = value
        copies = []
        for d in range(1, count):
            copy = pltpu.make_async_remote_copy(
                src_ref=held.at[base], dst_ref=slots.at[base + me],
                send_sem=send_sem.at[base + d], recv_sem=recv_sem.at[base + me],
                device_id=device(lax.rem(me + d, count)), device_id_type=MESH_IDS)
            copy.start()
            copies.append(copy)
        slots[base + me] = value
        for d in range(1, count):
            other = lax.rem(me + d, count)
            pltpu.make_async_remote_copy(
                src_ref=held.at[base], dst_ref=slots.at[base + other],
                send_sem=send_sem.at[base + d], recv_sem=recv_sem.at[base + other],
                device_id=device(other), device_id_type=MESH_IDS).wait_recv()
        value = slots[base]
        for i in range(1, count):
            value = value + slots[base + i]
        for copy in copies:
            copy.wait_send()
        base += count
    out_ref[...] = value


def all_sum(mesh, value):
    sizes = tuple(mesh.shape[name] for name in ('z', 'y', 'x', 'k'))
    slots = sizes[1] + sizes[2] * sizes[3] + sizes[0]
    tile = jnp.broadcast_to(value, (8, 128))
    out = pl.pallas_call(
        functools.partial(sum_kernel, sizes),
        out_shape=jax.ShapeDtypeStruct((8, 128), jnp.float32),
        in_specs=[pl.BlockSpec(memory_space=pltpu.VMEM)],
        out_specs=pl.BlockSpec(memory_space=pltpu.VMEM),
        scratch_shapes=[
            pltpu.VMEM((slots, 8, 128), jnp.float32),
            pltpu.VMEM((slots, 8, 128), jnp.float32),
            pltpu.SemaphoreType.DMA((slots,)),
            pltpu.SemaphoreType.DMA((slots,)),
        ],
        compiler_params=pltpu.CompilerParams(collective_id=0, has_side_effects=True),
    )(tile)
    return out[0, 0]


def solution(mesh):
    grid = fine_mesh(mesh)
    n_dev = grid.size
    n_y = grid.shape['y']

    def local_run(psi_blk, left_blk, right_blk, mpo_pair):
        num_elems = float(psi_blk.size * n_dev)
        rows = psi_blk.shape[0] // n_y
        mine = lax.axis_index('y') * rows
        left_rows = lax.dynamic_slice_in_dim(left_blk, mine, rows, 0)
        full_len = left_blk.shape[2]
        parts = (rows, left_blk.shape[1], grid.shape['x'], grid.shape['k'], n_y, rows)
        left_rows = left_rows.reshape(parts).transpose(0, 1, 4, 2, 3, 5).reshape(rows, left_blk.shape[1], full_len)
        right_rows = lax.all_gather(right_blk, 'y', axis=0, tiled=True)

        def mean_dot(left_vec, right_vec):
            return all_sum(grid, jnp.sum(left_vec * right_vec)) / num_elems

        def apply_ham(vec_blk):
            gathered = lax.all_gather(vec_blk, ('y', 'x', 'k'), axis=0, tiled=True)
            stage_one = jnp.einsum('cla,asub->lcsub', left_rows, gathered, precision=FULL_PREC, preferred_element_type=jnp.float32)
            stage_two = jnp.einsum('lrsutq,lcsub->rctqb', mpo_pair, stage_one, precision=FULL_PREC, preferred_element_type=jnp.float32)
            part_out = jnp.einsum('rctqb,bre->ctqe', stage_two, right_rows, precision=FULL_PREC, preferred_element_type=jnp.float32)
            return lax.psum_scatter(part_out, 'z', scatter_dimension=3, tiled=True)

        start = lax.all_to_all(psi_blk, 'y', 0, 3, tiled=True)
        cur_vec = start * lax.rsqrt(mean_dot(psi_blk, psi_blk))
        prev_vec = cur_vec
        alpha_list = []
        beta_list = []
        for step_idx in range(LANCZOS_STEPS):
            h_vec = apply_ham(cur_vec)
            alpha_j = mean_dot(cur_vec, h_vec)
            residual = h_vec - alpha_j * cur_vec
            if step_idx > 0:
                residual = residual - beta_list[-1] * prev_vec
            beta_j = jnp.sqrt(mean_dot(residual, residual))
            alpha_list.append(alpha_j)
            beta_list.append(beta_j)
            prev_vec = cur_vec
            cur_vec = residual / beta_j
        result = lax.all_to_all(cur_vec, 'y', 3, 0, tiled=True)
        return jnp.stack(alpha_list), jnp.stack(beta_list), result

    return jax.shard_map(
        local_run, mesh=grid,
        in_specs=(P(('x', 'k'), None, None, ('z', 'y')), P(('x', 'k'), None, None), P(('z', 'y'), None, None), P()),
        out_specs=(P(), P(), P(('x', 'k'), None, None, ('z', 'y'))), check_vma=False)
```

time: 2340 us -> 1120 us (0.48)
  blocking collectives: 869 us -> 0 us
  waiting for transfers between devices: 1110 us -> 618 us
  Pallas kernels: 0 us -> 156 us
  matrix products: 261 us -> 229 us
  local copies, waits for them, and re-layouts: 32.3 us -> 56.8 us
    psum x9 -> x0, blocking collectives: 869 us -> none  [mean_dot(): return lax.psum(jnp.sum(left_vec * right_vec), ('col', 'row')) / num_elems]
    reduce_scatter x4, waiting for transfers between devices: 992 us -> 239 us  [apply_ham(): return lax.psum_scatter(part_out, 'z', scatter_dimension=3, tiled=True)]
    all_gather x4 -> x5, waiting for transfers between devices: 116 us -> 370 us  [the longest x4 298 us: apply_ham(): gathered = lax.all_gather(vec_blk, ('y', 'x', 'k'), axis=0, tiled=True)]
    pallas_call x0 -> x9, Pallas kernels: none -> 156 us  [all_sum(): pl.pallas_call(functools.partial(sum_kernel, sizes), out_shape=jax.ShapeD...]
    dot_general x8, matrix products: 230 us -> 196 us  [the longest x4 100 us: apply_ham(): jnp.einsum('rctqb,bre->ctqe', stage_two, right_rows, precision=FULL_PREC,...]
  transfers between devices with their start and end apart: 9 -> 11, of which waited for: 8 -> 10; matrix products, arithmetic and copies ran while one was open for 1% -> 5% of each run, Pallas kernels for 0% -> 2%
where the time goes in v1:
time: 1120 us; the launch traced here: 1110 us
  waiting for transfers between devices  618 us (55%)
  matrix products  229 us (20%)
  Pallas kernels  156 us (14%)
  local copies, waits for them, and re-layouts  56.8 us (5%)
  other arithmetic  24.6 us (2%)
  between operations  20.7 us (2%)
    all_gather x4, waiting for transfers between devices, apply_ham(): gathered = lax.all_gather(vec_blk, ('y', 'x', 'k'), axis=0, tiled=True)  298 us
    reduce_scatter x4, waiting for transfers between devices, apply_ham(): return lax.psum_scatter(part_out, 'z', scatter_dimension=3, tiled=True)  239 us
    pallas_call x9, Pallas kernels, all_sum(): pl.pallas_call(functools.partial(sum_kernel, sizes), out_shape=jax.ShapeD...  156 us
    dot_general x4, matrix products, apply_ham(): jnp.einsum('rctqb,bre->ctqe', stage_two, right_rows, precision=FULL_PREC,...  100 us
    dot_general x4, matrix products, apply_ham(): jnp.einsum('cla,asub->lcsub', left_rows, gathered, precision=FULL_PREC, p...  96 us
    all_gather x1, waiting for transfers between devices, local_run(): right_rows = lax.all_gather(right_blk, 'y', axis=0, tiled=True)  71.8 us
    dot_general x4, matrix products, apply_ham(): jnp.einsum('lrsutq,lcsub->rctqb', mpo_pair, stage_one, precision=FULL_PRE...  32.7 us
  transfers between devices with their start and end apart: 11, of which 10 were waited for; matrix products, arithmetic and copies ran while one was open for 5% of the time, Pallas kernels for 2%

profile of v1, /device:TPU:1, one launch (start us, length us, event | category | flops | bytes accessed | tf_op | source)
XLA Modules:
  0.0 1114.5 jit_solution(1433000552462786509)
XLA Ops:
  8.9 1.9 reshape.72
  10.8 5.0 all-to-all-start
  17.8 22.6 %shard_map.67 = f32[8,128]{1,0:T(8,128)} custom-call(f32[8,128]{1,0:T(8,128)} %broadcast_in_dim.27.val_ref), custom_call_target="tpu_custom_call" | custom-call | tf_op jit(solution)/shard_map/pallas_call | solution.py:72
  42.9 2.3 reduce
  49.7 1.9 constant_dynamic-slice_fusion
  51.6 5.1 reshape.47
  56.6 7.7 copy.28
  64.3 6.4 reshape.50
  71.4 56.2 %all-gather.6.cloned.1.call-done = f32[2048,3,3,256]{3,0,2,1:T(8,128)} async-done(((f32[64,3,3,256]{3,0,2,1:T(8,128)}), f32[2048,3,3,256]{3,0,2,1:T(8,128)}) %all-gather.6.cloned.1.call-update) | async-done | bytes 18874384 | tf_op jit(solution)/shard_map/all_gather | solution.py:107
  127.6 23.5 %fusion.56 = f32[5,64,3,3,256,1,1]{4,1,0,3,2,6,5:T(8,128)S(1)} fusion(f32[64,5,2048,1,1]{2,0,1,3,4:T(8,128)S(1)} %reshape.50, f32[2048,3,3,256]{3,0,2,1:T(8,128)} %all-gather.6.cloned.1.call-done), kind=kOutput, calls=%fused_computation.40 | convolution fusion | flops 18119393280 | bytes 24444928 | tf_op jit(solution)/shard_map/cla,asub->lcsub/dot_general | solution.py:108
  151.1 9.2 fusion.44
  160.3 71.8 %all-gather.8.cloned.1.call-done = f32[256,5,2048]{2,0,1:T(8,128)} async-done(((f32[64,5,2048]{2,0,1:T(8,128)}), f32[256,5,2048]{2,0,1:T(8,128)}) %all-gather.8.cloned.1.call-update) | async-done | bytes 10485776 | tf_op jit(solution)/shard_map/all_gather | solution.py:101
  232.1 25.9 %fusion.24 = f32[64,3,3,2048]{3,0,2,1:T(8,128)} fusion(f32[256,5,2048]{2,0,1:T(8,128)} %all-gather.8.cloned.1.call-done, f32[5,64,3,3,256]{4,0,3,2,1:T(8,128)} %fusion.44), kind=kOutput, calls=%fused_computation.24 | convolution fusion | flops 18119393280 | bytes 18153472 | tf_op jit(solution)/shard_map/rctqb,bre->ctqe/dot_general | solution.py:110
  258.1 61.4 %reduce-scatter.5.cloned.1.call-done = f32[64,3,3,256]{3,0,2,1:T(8,128)} async-done(((f32[64,3,3,2048]{3,0,2,1:T(8,128)}), f32[64,3,3,256]{3,0,2,1:T(8,128)}) %reduce-scatter.5.cloned.1.call-update) | async-done | bytes 589840 | tf_op jit(solution)/shard_map/reduce_scatter | solution.py:111
  322.5 18.3 %shard_map.68 = f32[8,128]{1,0:T(8,128)} custom-call(f32[8,128]{1,0:T(8,128)} %broadcast_in_dim.28.val_ref), custom_call_target="tpu_custom_call" | custom-call | tf_op jit(solution)/shard_map/pallas_call | solution.py:72
  342.7 1.8 multiply_reduce_fusion.6
  345.8 15.1 %shard_map.69 = f32[8,128]{1,0:T(8,128)} custom-call(f32[8,128]{1,0:T(8,128)} %broadcast_in_dim.29.val_ref), custom_call_target="tpu_custom_call" | custom-call | tf_op jit(solution)/shard_map/pallas_call | solution.py:72
  362.8 2.0 broadcast_divide_fusion.3
  364.8 80.7 %all-gather.10.cloned.1.call-done = f32[2048,3,3,256]{3,0,2,1:T(8,128)} async-done(((f32[64,3,3,256]{3,0,2,1:T(8,128)}), f32[2048,3,3,256]{3,0,2,1:T(8,128)}) %all-gather.10.cloned.1.call-update) | async-done | bytes 18874384 | tf_op jit(solution)/shard_map/all_gather | solution.py:107
  445.5 24.1 %fusion.61 = f32[5,64,3,3,256,1,1]{4,1,0,3,2,6,5:T(8,128)S(1)} fusion(f32[64,5,2048,1,1]{2,0,1,3,4:T(8,128)} %copy-done.2, f32[2048,3,3,256]{3,0,2,1:T(8,128)} %all-gather.10.cloned.1.call-done), kind=kOutput, calls=%fused_computation.41 | convolution fusion | flops 18119393280 | bytes 24444928 | tf_op jit(solution)/shard_map/cla,asub->lcsub/dot_general | solution.py:108
  469.6 7.8 fusion.47
  477.4 24.8 %fusion.27 = f32[64,3,3,2048]{3,0,2,1:T(8,128)} fusion(f32[256,5,2048]{2,0,1:T(8,128)} %all-gather.8.cloned.1.call-done, f32[5,64,3,3,256]{4,0,3,2,1:T(8,128)S(1)} %fusion.47), kind=kOutput, calls=%fused_computation.25 | convolution fusion | flops 18119393280 | bytes 18153472 | tf_op jit(solution)/shard_map/rctqb,bre->ctqe/dot_general | solution.py:110
  502.3 59.2 %reduce-scatter.7.cloned.1.call-done = f32[64,3,3,256]{3,0,2,1:T(8,128)} async-done(((f32[64,3,3,2048]{3,0,2,1:T(8,128)}), f32[64,3,3,256]{3,0,2,1:T(8,128)}) %reduce-scatter.7.cloned.1.call-update) | async-done | bytes 589840 | tf_op jit(solution)/shard_map/reduce_scatter | solution.py:111
  564.6 18.3 %shard_map.70 = f32[8,128]{1,0:T(8,128)} custom-call(f32[8,128]{1,0:T(8,128)} %broadcast_in_dim.30.val_ref), custom_call_target="tpu_custom_call" | custom-call | tf_op jit(solution)/shard_map/pallas_call | solution.py:72
  584.8 1.8 multiply_reduce_fusion.4
  587.8 15.1 %shard_map.71 = f32[8,128]{1,0:T(8,128)} custom-call(f32[8,128]{1,0:T(8,128)} %broadcast_in_dim.31.val_ref), custom_call_target="tpu_custom_call" | custom-call | tf_op jit(solution)/shard_map/pallas_call | solution.py:72
  605.8 80.7 %all-gather.12.cloned.1.call-done = f32[2048,3,3,256]{3,0,2,1:T(8,128)} async-done(((f32[64,3,3,256]{3,0,2,1:T(8,128)}), f32[2048,3,3,256]{3,0,2,1:T(8,128)}) %all-gather.12.cloned.1.call-update) | async-done | bytes 18874384 | tf_op jit(solution)/shard_map/all_gather | solution.py:107
  686.5 24.3 %fusion.66 = f32[5,64,3,3,256,1,1]{4,1,0,3,2,6,5:T(8,128)S(1)} fusion(f32[64,5,2048,1,1]{2,0,1,3,4:T(8,128)} %copy-done.2, f32[2048,3,3,256]{3,0,2,1:T(8,128)} %all-gather.12.cloned.1.call-done), kind=kOutput, calls=%fused_computation.42 | convolution fusion | flops 18119393280 | bytes 24444928 | tf_op jit(solution)/shard_map/cla,asub->lcsub/dot_general | solution.py:108
  710.8 7.8 fusion.50
  718.6 24.8 %fusion.30 = f32[64,3,3,2048]{3,0,2,1:T(8,128)} fusion(f32[256,5,2048]{2,0,1:T(8,128)} %all-gather.8.cloned.1.call-done, f32[5,64,3,3,256]{4,0,3,2,1:T(8,128)S(1)} %fusion.50), kind=kOutput, calls=%fused_computation.26 | convolution fusion | flops 18119393280 | bytes 18153472 | tf_op jit(solution)/shard_map/rctqb,bre->ctqe/dot_general | solution.py:110
  743.4 59.2 %reduce-scatter.9.cloned.1.call-done = f32[64,3,3,256]{3,0,2,1:T(8,128)} async-done(((f32[64,3,3,2048]{3,0,2,1:T(8,128)}), f32[64,3,3,256]{3,0,2,1:T(8,128)}) %reduce-scatter.9.cloned.1.call-update) | async-done | bytes 589840 | tf_op jit(solution)/shard_map/reduce_scatter | solution.py:111
  802.7 1.8 multiply_reduce_fusion.3
  805.8 18.3 %shard_map.72 = f32[8,128]{1,0:T(8,128)} custom-call(f32[8,128]{1,0:T(8,128)} %broadcast_in_dim.32.val_ref), custom_call_target="tpu_custom_call" | custom-call | tf_op jit(solution)/shard_map/pallas_call | solution.py:72
  825.9 1.8 multiply_reduce_fusion.2
  829.0 15.1 %shard_map.73 = f32[8,128]{1,0:T(8,128)} custom-call(f32[8,128]{1,0:T(8,128)} %broadcast_in_dim.33.val_ref), custom_call_target="tpu_custom_call" | custom-call | tf_op jit(solution)/shard_map/pallas_call | solution.py:72
  847.0 80.7 %all-gather.14.cloned.1.call-done = f32[2048,3,3,256]{3,0,2,1:T(8,128)} async-done(((f32[64,3,3,256]{3,0,2,1:T(8,128)}), f32[2048,3,3,256]{3,0,2,1:T(8,128)}) %all-gather.14.cloned.1.call-update) | async-done | bytes 18874384 | tf_op jit(solution)/shard_map/all_gather | solution.py:107
  927.6 24.1 %fusion.71 = f32[5,64,3,3,256,1,1]{4,1,0,3,2,6,5:T(8,128)S(1)} fusion(f32[64,5,2048,1,1]{2,0,1,3,4:T(8,128)} %copy-done.2, f32[2048,3,3,256]{3,0,2,1:T(8,128)} %all-gather.14.cloned.1.call-done), kind=kOutput, calls=%fused_computation.43 | convolution fusion | flops 18119393280 | bytes 24444928 | tf_op jit(solution)/shard_map/cla,asub->lcsub/dot_general | solution.py:108
  951.8 7.8 fusion.53
  959.6 24.8 %fusion.33 = f32[64,3,3,2048]{3,0,2,1:T(8,128)} fusion(f32[256,5,2048]{2,0,1:T(8,128)} %all-gather.8.cloned.1.call-done, f32[5,64,3,3,256]{4,0,3,2,1:T(8,128)S(1)} %fusion.53), kind=kOutput, calls=%fused_computation.27 | convolution fusion | flops 18119393280 | bytes 18153472 | tf_op jit(solution)/shard_map/rctqb,bre->ctqe/dot_general | solution.py:110
  984.5 59.3 %reduce-scatter.11.cloned.1.call-done = f32[64,3,3,256]{3,0,2,1:T(8,128)} async-done(((f32[64,3,3,2048]{3,0,2,1:T(8,128)}), f32[64,3,3,256]{3,0,2,1:T(8,128)}) %reduce-scatter.11.cloned.1.call-update) | async-done | bytes 589840 | tf_op jit(solution)/shard_map/reduce_scatter | solution.py:111
  1043.8 1.8 multiply_reduce_fusion.1
  1046.8 18.3 %shard_map.74 = f32[8,128]{1,0:T(8,128)} custom-call(f32[8,128]{1,0:T(8,128)} %broadcast_in_dim.34.val_ref), custom_call_target="tpu_custom_call" | custom-call | tf_op jit(solution)/shard_map/pallas_call | solution.py:72
  1067.0 1.8 multiply_reduce_fusion
  1070.1 15.1 %shard_map.75 = f32[8,128]{1,0:T(8,128)} custom-call(f32[8,128]{1,0:T(8,128)} %broadcast_in_dim.35.val_ref), custom_call_target="tpu_custom_call" | custom-call | tf_op jit(solution)/shard_map/pallas_call | solution.py:72
  1087.9 1.9 reshape.74
  1089.8 3.8 all-to-all-start.1
  1094.2 7.8 all-to-all-done.1
  1102.0 2.3 reduce.1
  (65 shorter events, 40.3 us)
Async XLA Ops:
  7.2 8.7 copy-start.3
  10.8 31.5 %all-to-all-start = ((f32[4,1,36864]{2,1,0:T(1,128)}), f32[4,1,36864]{2,1,0:T(1,128)S(1)}, u32[]{:S(2)}, u32[]{:S(2)}) async-start(f32[4,1,36864]{2,1,0:T(1,128)} %reshape.72), calls=%async_computation | async-start | bytes 1179648 | tf_op jit(solution)/shard_map/all_to_all | solution.py:113
  15.8 111.8 %all-gather.6.cloned.1.call-start = ((), (), s32[]{:S(2)}) async-start(), calls=%async_computation.6 | async-start | bytes 19464192 | tf_op jit(solution)/shard_map/all_gather | solution.py:107
  48.6 183.5 %all-gather.8.cloned.1.call-start = ((), (), s32[]{:S(2)}) async-start(), calls=%async_computation.7 | async-start | bytes 13107200 | tf_op jit(solution)/shard_map/all_gather | solution.py:101
  49.4 270.1 %reduce-scatter.5.cloned.1.call-start = ((), (), s32[]{:S(2)}) async-start(), calls=%async_computation.8 | async-start | bytes 5308416 | tf_op jit(solution)/shard_map/reduce_scatter | solution.py:111
  64.3 6.4 copy-start.4
  70.8 80.4 %copy-start.2 = (f32[64,5,2048,1,1]{2,0,1,3,4:T(8,128)}, f32[64,5,2048,1,1]{2,0,1,3,4:T(8,128)S(1)}, u32[]{:S(2)}) copy-start(f32[64,5,2048,1,1]{2,0,1,3,4:T(8,128)S(1)} %reshape.50) | copy-start | bytes 7864324
  258.0 61.5 %copy-start = (f32[64,3,3,256]{3,0,2,1:T(8,128)S(1)}, f32[64,3,3,256]{3,0,2,1:T(8,128)}, u32[]{:S(2)}) copy-start(f32[64,3,3,256]{3,0,2,1:T(8,128)} %mul.86) | copy-start | bytes 1769476
  258.1 187.4 %all-gather.10.cloned.1.call-start = ((), (), s32[]{:S(2)}) async-start(), calls=%async_computation.9 | async-start | bytes 19464192 | tf_op jit(solution)/shard_map/all_gather | solution.py:107
  364.8 196.8 %reduce-scatter.7.cloned.1.call-start = ((), (), s32[]{:S(2)}) async-start(), calls=%async_computation.10 | async-start | bytes 5308416 | tf_op jit(solution)/shard_map/reduce_scatter | solution.py:111
  502.2 59.3 %copy-start.1 = (f32[64,3,3,256]{3,0,2,1:T(8,128)S(1)}, f32[64,3,3,256]{3,0,2,1:T(8,128)}, u32[]{:S(2)}) copy-start(f32[64,3,3,256]{3,0,2,1:T(8,128)} %broadcast_divide_fusion.3) | copy-start | bytes 1769476
  502.2 184.2 %all-gather.12.cloned.1.call-start = ((), (), s32[]{:S(2)}) async-start(), calls=%async_computation.11 | async-start | bytes 19464192 | tf_op jit(solution)/shard_map/all_gather | solution.py:107
  605.7 197.0 %reduce-scatter.9.cloned.1.call-start = ((), (), s32[]{:S(2)}) async-start(), calls=%async_computation.12 | async-start | bytes 5308416 | tf_op jit(solution)/shard_map/reduce_scatter | solution.py:111
  743.4 184.2 %all-gather.14.cloned.1.call-start = ((), (), s32[]{:S(2)}) async-start(), calls=%async_computation.13 | async-start | bytes 19464192 | tf_op jit(solution)/shard_map/all_gather | solution.py:107
  846.9 196.9 %reduce-scatter.11.cloned.1.call-start = ((), (), s32[]{:S(2)}) async-start(), calls=%async_computation.14 | async-start | bytes 5308416 | tf_op jit(solution)/shard_map/reduce_scatter | solution.py:111
  1089.8 12.2 %all-to-all-start.1 = ((f32[4,1,36864]{2,1,0:T(1,128)}), f32[4,1,36864]{2,1,0:T(1,128)S(1)}, u32[]{:S(2)}, u32[]{:S(2)}) async-start(f32[4,1,36864]{2,1,0:T(1,128)} %reshape.74), calls=%async_computation.5 | async-start | bytes 1179648 | tf_op jit(solution)/shard_map/all_to_all | solution.py:129
Sparse Core Ops, SparseCore 0:
  48.8 78.8 all-gather.5
  129.4 102.5 all-gather.7
  258.2 61.2 reduce-scatter.4
  364.9 80.5 all-gather.9
  502.4 59.1 reduce-scatter.6
  605.8 80.5 all-gather.11
  743.5 59.1 reduce-scatter.8
  847.0 80.5 all-gather.13
  984.6 59.1 reduce-scatter.10

commit v2 on v0

v2 whole, which is shorter than its diff:
```python
import functools
import itertools

import jax
import jax.numpy as jnp
from jax import lax
from jax.experimental import pallas as pl
from jax.experimental.pallas import tpu as pltpu
from jax.sharding import Mesh, PartitionSpec as P

LANCZOS_STEPS = 4
FULL_PREC = lax.Precision.HIGHEST
MESH_IDS = pl.DeviceIdType.MESH
RING = 4
CORES = 2
PARTS = 4
NUM_SLOTS = RING * RING


def fine_mesh(mesh):
    shape = (mesh.shape['col'] // RING, RING, mesh.shape['row'] // CORES, CORES)
    return Mesh(mesh.devices.reshape(shape), ('z', 'y', 'x', 'k'))


def tree_axes(part):
    return ('x', 'y') if part < 2 else ('y', 'x')


def tree_sends(part, df, ds):
    first, second = tree_axes(part)
    way = 1 if part % 2 == 0 else -1
    sends = []
    if ds == 0:
        if df == 0:
            sends += [((first, 1), (part, 3, 0)), ((first, -1), (part, 1, 0))]
        if df == (3 if way == 1 else 1):
            sends.append(((first, way), (part, 2, 0)))
        sends += [((second, 1), (part, df, 3)), ((second, -1), (part, df, 1))]
    if ds == (3 if way == 1 else 1):
        sends.append(((second, way), (part, df, 2)))
    return sends


def slot_xy(message):
    part, df, ds = message
    return (df, ds) if part < 2 else (ds, df)


def gather_order():
    free = {link: 0.0 for link in itertools.product('xy', (1, -1))}
    arrival = {}

    def issue(now, sends):
        for link, message in sends:
            free[link] = max(free[link], now) + 1.0
            arrival[message] = free[link] + 0.6

    own = [tree_sends(part, 0, 0) for part in range(PARTS)]
    issue(0.0, [s for sends in own for s in sends[:2]])
    issue(0.0, [s for sends in own for s in sends[2:]])
    order = []
    while len(order) < 15 * PARTS:
        now, message = min((t, m) for m, t in arrival.items() if m not in order)
        order.append(message)
        issue(now, tree_sends(*message))
    return order


ORDER = gather_order()
NUM_MSGS = len(ORDER)
GROUPS = [ORDER[i:i + 4] for i in range(0, NUM_MSGS, 4)]
LAST_GROUP = {}
for group_idx, group in enumerate(GROUPS):
    for message in group:
        LAST_GROUP[slot_xy(message)] = group_idx
SLOTS = [(0, 0)] + sorted(LAST_GROUP, key=lambda xy: (LAST_GROUP[xy], xy))
CHUNK = 4
NUM_CHUNKS = NUM_SLOTS // CHUNK


def dot(lhs, rhs):
    return jnp.dot(lhs, rhs, precision=FULL_PREC, preferred_element_type=jnp.float32)


def lanczos_kernel(
        num_elems, num_z, psi_ref, left_ref, right_ref, w_ref, out_ref, scal_ref,
        gath, right_full, left_own, left_perm, acc, mid, ring, part_sum, h_buf, v_buf, turn_in, turn_mid, turn_out,
        red_held, red_slots,
        ag_send, ag_recv, sib_send, sib_recv, rs_send, rs_recv, red_send, red_recv, turn_send, turn_recv,
        env_send, env_recv, load_sem, ag_credit, rs_credit):
    phys, rows, cols = h_buf.shape[1:]
    bonds = right_full.shape[0]
    piece = rows // PARTS
    octs = rows // 8
    z, y, x, k = (lax.axis_index(name) for name in ('z', 'y', 'x', 'k'))
    xk = x * CORES + k
    other = 1 - k

    def step_to(axis, sign):
        pos = {'x': x, 'y': y}[axis]
        return {axis: lax.rem(pos + RING + sign, RING)}

    phases = (
        (num_z, z, lambda i: {'z': i}),
        (RING, y, lambda i: {'y': i}),
        (RING * CORES, xk, lambda i: {'x': i // CORES, 'k': lax.rem(i, CORES)}),
    )
    bases = (0, num_z, num_z + RING)
    barrier = pltpu.get_barrier_semaphore()
    total = 0
    for count, me, device in phases:
        for d in range(1, count):
            pl.semaphore_signal(barrier, inc=1, device_id=device(lax.rem(me + d, count)), device_id_type=MESH_IDS)
            total += 1

    load_left = pltpu.make_async_copy(
        left_ref.at[:, pl.ds(pl.multiple_of(y * rows, rows), rows), :], left_own, load_sem.at[0])
    load_left.start()
    own_rows = pl.multiple_of(y * rows, rows)
    load_right = pltpu.make_async_copy(right_ref, right_full.at[:, pl.ds(own_rows, rows), :], load_sem.at[1])
    load_right.start()
    pl.semaphore_wait(barrier, total)

    def sum_start(which, phase, value):
        count, me, device = phases[phase]
        red_held[which, phase] = value
        for d in range(1, count):
            pltpu.make_async_remote_copy(
                src_ref=red_held.at[which, phase], dst_ref=red_slots.at[which, bases[phase] + me],
                send_sem=red_send.at[which, bases[phase] + d], recv_sem=red_recv.at[which, bases[phase] + me],
                device_id=device(lax.rem(me + d, count)), device_id_type=MESH_IDS).start()
        red_slots[which, bases[phase] + me] = value

    def sum_finish(which, phase):
        count, me, device = phases[phase]
        for d in range(1, count):
            peer = lax.rem(me + d, count)
            copy = pltpu.make_async_remote_copy(
                src_ref=red_held.at[which, phase], dst_ref=red_slots.at[which, bases[phase] + peer],
                send_sem=red_send.at[which, bases[phase] + d], recv_sem=red_recv.at[which, bases[phase] + peer],
                device_id=device(peer), device_id_type=MESH_IDS)
            copy.wait_send()
            copy.wait_recv()
        value = red_slots[which, bases[phase]]
        for i in range(1, count):
            value = value + red_slots[which, bases[phase] + i]
        return value

    def mean_of(value):
        return jnp.broadcast_to(jnp.sum(value, axis=(0, 1), keepdims=True) * (1.0 / num_elems), (8, 128))

    def fold(values):
        lanes = values.reshape(-1, 8, cols).sum(0)
        tile = lanes[:, :128]
        for c in range(128, cols, 128):
            tile = tile + lanes[:, c:c + 128]
        return tile

    def gather_copy(link, message):
        axis, sign = link
        dx, dy = slot_xy(message)
        sx = (dx + sign) % RING if axis == 'x' else dx
        sy = (dy + sign) % RING if axis == 'y' else dy
        index = ORDER.index(message)
        span = pl.ds(message[0] * piece, piece)
        return pltpu.make_async_remote_copy(
            src_ref=gath.at[0, SLOTS.index((sx, sy)), :, span, :], dst_ref=gath.at[0, SLOTS.index((dx, dy)), :, span, :],
            send_sem=ag_send.at[index], recv_sem=ag_recv.at[index],
            device_id=step_to(axis, sign), device_id_type=MESH_IDS)

    all_sends = {}
    for message in [(part, 0, 0) for part in range(PARTS)] + ORDER:
        for link, sent in tree_sends(*message):
            all_sends[sent] = link

    def sibling_copy(slot):
        return pltpu.make_async_remote_copy(
            src_ref=gath.at[0, slot], dst_ref=gath.at[1, slot],
            send_sem=sib_send.at[slot], recv_sem=sib_recv.at[slot],
            device_id={'k': other}, device_id_type=MESH_IDS)

    def send_own(part):
        for link, sent in tree_sends(part, 0, 0):
            gather_copy(link, sent).start()

    def turn_copy(src, dst, index, d, device):
        return pltpu.make_async_remote_copy(
            src_ref=src, dst_ref=dst, send_sem=turn_send.at[d], recv_sem=turn_recv.at[index],
            device_id=device, device_id_type=MESH_IDS)

    per_tile = 128 // rows
    for d in range(1, RING):
        peer = lax.rem(y + d, RING)
        lanes = pl.ds(pl.multiple_of((peer // per_tile) * 128, 128), 128)
        turn_copy(psi_ref.at[:, :, lanes], turn_in.at[y], y, d, {'y': peer}).start()
    turn_in[y] = psi_ref[:, :, pl.ds(pl.multiple_of((y // per_tile) * 128, 128), 128)]
    h_buf[1] = jnp.zeros(h_buf.shape[1:], jnp.float32)
    v_buf[...] = jnp.zeros(v_buf.shape, jnp.float32)
    for d in range(1, RING):
        peer = lax.rem(y + d, RING)
        copy = turn_copy(psi_ref.at[:, :, pl.ds(0, 128)], turn_in.at[peer], peer, d, {'y': peer})
        copy.wait_send()
        copy.wait_recv()
    sub = pl.ds(pl.multiple_of(lax.rem(y, per_tile) * rows, rows), rows)

    def turn_body(p, c):
        block = jnp.concatenate([turn_in[i, p] for i in range(RING)], axis=0)
        turn_mid[0] = jnp.transpose(block)
        mine = turn_mid[0, sub, :]
        h_buf[0, p] = mine
        gath[0, 0, p] = mine
        return c

    lax.fori_loop(0, phys, turn_body, 0)
    for part in range(PARTS):
        send_own(part)
    sibling_copy(0).start()

    load_left.wait()
    bonds_l = left_own.shape[0]
    lane = lax.broadcasted_iota(jnp.int32, (bonds_l * rows, 128), 1)
    for tile in range(left_perm.shape[1] // 128):
        halves = []
        for h in range(2):
            column = tile * 128 + h * rows
            chunk, rest = divmod(column, CHUNK * CORES * rows)
            dk, rest = divmod(rest, CHUNK * rows)
            dx, dy = SLOTS[chunk * CHUNK + rest // rows]
            block = (lax.rem(x + dx, RING) * CORES + lax.rem(k + dk, CORES)) * RING + lax.rem(y + dy, RING)
            first = pl.multiple_of((block // 2) * 128, 128)
            values = left_own[:, :, pl.ds(first, 128)].reshape(bonds_l * rows, 128)
            halves.append(jnp.where(lax.rem(block, 2) == h, values, pltpu.roll(values, rows, 1)))
        left_perm[:, tile * 128:(tile + 1) * 128] = jnp.where(lane < rows, halves[0], halves[1])

    def stage_one(chunk, lo, hi):
        def body(p, c):
            rhs = jnp.concatenate(
                [gath[dk, chunk * CHUNK + i, p] for dk in range(CORES) for i in range(CHUNK)], axis=0)
            depth = CHUNK * CORES * rows
            res = dot(left_perm[:, chunk * depth:(chunk + 1) * depth], rhs).reshape(bonds_l, octs, 8, cols)
            if chunk == 0:
                acc[p] = res
            else:
                acc[p] = acc[p] + res
            return c
        lax.fori_loop(lo, hi, body, 0)

    def wait_sibling(chunk):
        for i in range(CHUNK):
            sibling_copy(chunk * CHUNK + i).wait_recv()

    half = rows // 2
    quarter = rows // 4

    def env_view(row, count, i):
        off = jnp.where(lax.rem(i, 2) == 0, -(i // 2 + 1), i // 2 + 1) * jnp.where(i == num_z - 1, 0, 1)
        block = lax.rem(z + num_z + off, num_z)
        return right_full.at[:, pl.ds(pl.multiple_of(row, 8), count), pl.ds(pl.multiple_of(block * cols, cols), cols)]

    def env_copy(kind, i, row, count, device):
        view = env_view(row, count, i)
        return pltpu.make_async_remote_copy(
            src_ref=view, dst_ref=view, send_sem=env_send.at[kind, i], recv_sem=env_recv.at[kind, i],
            device_id=device, device_id_type=MESH_IDS)

    up, down, far = (lax.rem(y + d, RING) for d in (1, 3, 2))

    def env_row(owner, core):
        return owner * rows + core * half

    def env_start(i, c):
        env_copy(0, i, env_row(y, k), half, {'y': up}).start()
        env_copy(1, i, env_row(y, k), half, {'y': down}).start()
        return c

    def env_pass(i, c):
        env_copy(0, i, env_row(down, k), half, {'y': up}).wait_recv()
        env_copy(2, i, env_row(down, k), quarter, {'y': up}).start()
        env_copy(4, i, env_row(down, k), half, {'k': other}).start()
        env_copy(1, i, env_row(up, k), half, {'y': down}).wait_recv()
        env_copy(3, i, env_row(up, k) + quarter, quarter, {'y': down}).start()
        env_copy(5, i, env_row(up, k), half, {'k': other}).start()
        return c

    def env_end(i, c):
        env_copy(2, i, env_row(far, k), quarter, {'y': up}).wait_recv()
        env_copy(3, i, env_row(far, k) + quarter, quarter, {'y': down}).wait_recv()
        env_copy(6, i, env_row(far, k), half, {'k': other}).start()
        return c

    def env_done(i, c):
        env_copy(4, i, env_row(down, other), half, {'k': other}).wait_recv()
        env_copy(5, i, env_row(up, other), half, {'k': other}).wait_recv()
        env_copy(6, i, env_row(far, other), half, {'k': other}).wait_recv()
        for kind, row, count in ((0, env_row(y, k), half), (1, env_row(y, k), half), (2, env_row(down, k), quarter),
                                 (3, env_row(up, k) + quarter, quarter), (4, env_row(down, k), half),
                                 (5, env_row(up, k), half), (6, env_row(far, k), half)):
            env_copy(kind, i, row, count, {'k': other}).wait_send()
        return c

    def way(s):
        return 1 - 2 * lax.rem(s, 2)

    def ring_block(s, t):
        return lax.rem(z + 2 * num_z - way(s) * (1 + t), num_z)

    def ring_copy(s, t):
        return pltpu.make_async_remote_copy(
            src_ref=ring.at[s, t], dst_ref=ring.at[s, t + 1], send_sem=rs_send.at[s, t], recv_sem=rs_recv.at[s, t + 1],
            device_id={'z': lax.rem(z + num_z + way(s), num_z)}, device_id_type=MESH_IDS)

    per_part = piece // 8

    def last_stage(s, t):
        lhs = mid[:, pl.ds(s * per_part, per_part)].reshape(phys * piece, bonds * cols)
        first = pl.multiple_of(ring_block(s, t) * cols, cols)
        rhs = right_full[:, :, pl.ds(first, cols)].reshape(bonds * cols, cols)
        return dot(lhs, rhs).reshape(phys, piece, cols)

    def ring_first(s, c):
        def middle(i, c2):
            o = s * per_part + i
            res = dot(w_ref[...], acc[:, :, o].reshape(phys * bonds_l * 8, cols)).reshape(bonds, phys, 8, cols)
            for r in range(bonds):
                mid[:, o, :, r * cols:(r + 1) * cols] = res[r]
            return c2
        lax.fori_loop(0, per_part, middle, 0)
        ring[s, 0] = last_stage(s, 0)
        ring_copy(s, 0).start()
        return c

    def ring_second(s, c):
        part_sum[s] = last_stage(s, 1)
        return c

    def ring_hop(i, c):
        t, s = 1 + i // PARTS, lax.rem(i, PARTS)
        ring_copy(s, t - 1).wait_recv()
        ring[s, t] = ring[s, t] + part_sum[s]
        ring_copy(s, t).start()
        part_sum[s] = last_stage(s, t + 1)
        return c

    def new_direction(cur, alpha, beta_prev):
        nxt = 1 - cur
        a, b = alpha[0:1, 0:1], beta_prev[0:1, 0:1]
        total = jnp.zeros((8, 128), jnp.float32)
        for p in range(phys):
            w = h_buf[cur, p] - a * v_buf[cur, p] - b * v_buf[nxt, p]
            v_buf[nxt, p] = w
            total = total + fold(w * w)
        return total

    def step(j, carry):
        alpha_part, beta_prev = carry
        cur = lax.rem(j, 2)
        nxt = 1 - cur
        sum_start(0, 0, alpha_part)
        state = {}
        for g, group in enumerate(GROUPS):
            for message in group:
                gather_copy(all_sends[message], message).wait_recv()
                for link, sent in tree_sends(*message):
                    gather_copy(link, sent).start()
            for xy, last in LAST_GROUP.items():
                if last == g:
                    sibling_copy(SLOTS.index(xy)).start()
            if g == 1:
                sum_start(0, 1, sum_finish(0, 0))
            if g == 4:
                wait_sibling(0)
            if g in (4, 5, 6):
                stage_one(0, (g - 4) * phys // 3, (g - 3) * phys // 3)
            if g == 6:
                sum_start(0, 2, sum_finish(0, 1))
            if g == 9:
                wait_sibling(1)
            if g in (9, 10, 11):
                stage_one(1, (g - 9) * phys // 3, (g - 8) * phys // 3)
            if g == 11:
                alpha = mean_of(sum_finish(0, 2))
                scal_ref[0, j] = alpha
                sum_start(1, 0, new_direction(cur, alpha, beta_prev))
            if g == 13:
                wait_sibling(2)
                stage_one(2, 0, phys // 3)
                sum_start(1, 1, sum_finish(1, 0))

        @pl.when(j == 0)
        def _():
            load_right.wait()
            lax.fori_loop(0, num_z, env_start, 0)

        stage_one(2, phys // 3, phys)
        wait_sibling(3)
        stage_one(3, 0, phys)
        for message, link in all_sends.items():
            gather_copy(link, message).wait_send()
        for slot in range(NUM_SLOTS):
            sibling_copy(slot).wait_send()

        @pl.when(j < LANCZOS_STEPS - 1)
        def _():
            for axis, sign in itertools.product('xy', (1, -1)):
                pl.semaphore_signal(ag_credit, inc=1, device_id=step_to(axis, sign), device_id_type=MESH_IDS)
            pl.semaphore_signal(ag_credit, inc=1, device_id={'k': other}, device_id_type=MESH_IDS)

        @pl.when(j == 0)
        def _():
            lax.fori_loop(0, num_z, env_pass, 0)
            lax.fori_loop(0, num_z, env_end, 0)
            lax.fori_loop(0, num_z, env_done, 0)

        @pl.when(j > 0)
        def _():
            pl.semaphore_wait(rs_credit, 2)

        lax.fori_loop(0, PARTS, ring_first, 0)
        sum_start(1, 2, sum_finish(1, 1))
        lax.fori_loop(0, PARTS, ring_second, 0)
        lax.fori_loop(0, PARTS * (num_z - 2), ring_hop, 0)
        beta = jnp.sqrt(mean_of(sum_finish(1, 2)))
        scal_ref[1, j] = beta

        @pl.when(j < LANCZOS_STEPS - 1)
        def _():
            pl.semaphore_wait(ag_credit, 5)

        alpha = scal_ref[0, j]
        a, b, inv = alpha[0:1, 0:1], beta_prev[0:1, 0:1], (1.0 / beta)[0:1, 0:1]
        new_part = jnp.zeros((8, 128), jnp.float32)
        for s in range(PARTS):
            ring_copy(s, num_z - 2).wait_recv()
            span = slice(s * piece, (s + 1) * piece)
            for p in range(phys):
                g_new = ring[s, num_z - 1, p] + part_sum[s, p]
                h_new = (g_new - a * h_buf[cur, p, span, :] - b * h_buf[nxt, p, span, :]) * inv
                v_new = v_buf[nxt, p, span, :] * inv
                h_buf[nxt, p, span, :] = h_new
                gath[0, 0, p, span, :] = h_new
                v_buf[nxt, p, span, :] = v_new
                new_part = new_part + fold(v_new * h_new)

            @pl.when(j < LANCZOS_STEPS - 1)
            def _():
                send_own(s)

        @pl.when(j < LANCZOS_STEPS - 1)
        def _():
            sibling_copy(0).start()

        for s in range(PARTS):
            for t in range(num_z - 1):
                ring_copy(s, t).wait_send()

        @pl.when(j < LANCZOS_STEPS - 1)
        def _():
            for sign in (1, num_z - 1):
                pl.semaphore_signal(
                    rs_credit, inc=1, device_id={'z': lax.rem(z + sign, num_z)}, device_id_type=MESH_IDS)

        return new_part, jnp.where(j > 0, beta, 0.0)

    zero = jnp.zeros((8, 128), jnp.float32)
    alpha_part, beta_prev = lax.fori_loop(0, LANCZOS_STEPS, step, (zero, zero))

    def sum_now(which, value):
        for phase in range(3):
            sum_start(which, phase, value)
            value = sum_finish(which, phase)
        return mean_of(value)

    cur = LANCZOS_STEPS % 2
    alpha = sum_now(0, alpha_part)
    scal_ref[0, LANCZOS_STEPS] = alpha
    beta = jnp.sqrt(sum_now(1, new_direction(cur, alpha, beta_prev)))
    scal_ref[1, LANCZOS_STEPS] = beta
    inv = (1.0 / beta)[0:1, 0:1]
    turn_mid[0] = jnp.zeros((128, RING * rows), jnp.float32)

    def unturn_body(p, c):
        turn_mid[0, sub, :] = v_buf[1 - cur, p] * inv
        turned = jnp.transpose(turn_mid[0])
        for i in range(RING):
            turn_out[i, p] = turned[i * rows:(i + 1) * rows, :]
        return c

    lax.fori_loop(0, phys, unturn_body, 0)
    for d in range(1, RING):
        peer = lax.rem(y + d, RING)
        turn_copy(turn_out.at[peer], turn_in.at[y], y, d, {'y': peer}).start()
    turn_in[y] = turn_out[y]
    for d in range(1, RING):
        peer = lax.rem(y + d, RING)
        copy = turn_copy(turn_out.at[peer], turn_in.at[peer], peer, d, {'y': peer})
        copy.wait_send()
        copy.wait_recv()
    first_lanes = lax.broadcasted_iota(jnp.int32, (phys, rows, 128), 2) < rows
    for pair in range(RING // per_tile):
        out_ref[:, :, pair * 128:(pair + 1) * 128] = jnp.where(first_lanes, turn_in[2 * pair], turn_in[2 * pair + 1])


def solution(mesh):
    grid = fine_mesh(mesh)
    num_z = grid.shape['z']

    def local_run(psi_blk, left_blk, right_blk, mpo_pair):
        full_rows, n_s, n_u, local_cols = psi_blk.shape
        phys = n_s * n_u
        rows = full_rows // RING
        cols = local_cols * RING
        bonds_l, bonds_r = left_blk.shape[1], right_blk.shape[1]
        full_a, full_b = left_blk.shape[2], right_blk.shape[2]
        psi = psi_blk.transpose(1, 2, 3, 0).reshape(phys, local_cols, full_rows)
        left = left_blk.transpose(1, 0, 2)
        right = right_blk.transpose(1, 0, 2)
        w_flat = mpo_pair.reshape(bonds_l, bonds_r, phys, phys).transpose(1, 3, 2, 0)
        w_flat = w_flat.reshape(bonds_r * phys, 1, phys * bonds_l, 1) * jnp.eye(8, dtype=jnp.float32)[None, :, None, :]
        w_flat = w_flat.reshape(bonds_r * phys * 8, phys * bonds_l * 8)
        red = num_z + RING + RING * CORES
        f32 = jnp.float32
        out, scal = pl.pallas_call(
            functools.partial(lanczos_kernel, float(psi_blk.size * grid.size), num_z),
            out_shape=(
                jax.ShapeDtypeStruct((phys, local_cols, full_rows), f32),
                jax.ShapeDtypeStruct((2, LANCZOS_STEPS + 1, 8, 128), f32),
            ),
            in_specs=[
                pl.BlockSpec(memory_space=pltpu.VMEM),
                pl.BlockSpec(memory_space=pl.ANY),
                pl.BlockSpec(memory_space=pl.ANY),
                pl.BlockSpec(memory_space=pltpu.VMEM),
            ],
            out_specs=(pl.BlockSpec(memory_space=pltpu.VMEM), pl.BlockSpec(memory_space=pltpu.VMEM)),
            scratch_shapes=[
                pltpu.VMEM((CORES, NUM_SLOTS, phys, rows, cols), f32),
                pltpu.VMEM((bonds_r, cols, full_b), f32),
                pltpu.VMEM((bonds_l, rows, full_a), f32),
                pltpu.VMEM((bonds_l * rows, full_a), f32),
                pltpu.VMEM((phys, bonds_l, rows // 8, 8, cols), f32),
                pltpu.VMEM((phys, rows // 8, 8, bonds_r * cols), f32),
                pltpu.VMEM((PARTS, num_z, phys, rows // PARTS, cols), f32),
                pltpu.VMEM((PARTS, phys, rows // PARTS, cols), f32),
                pltpu.VMEM((2, phys, rows, cols), f32),
                pltpu.VMEM((2, phys, rows, cols), f32),
                pltpu.VMEM((RING, phys, local_cols, 128), f32),
                pltpu.VMEM((1, 128, cols), f32),
                pltpu.VMEM((RING, phys, local_cols, 128), f32),
                pltpu.VMEM((2, 3, 8, 128), f32),
                pltpu.VMEM((2, red, 8, 128), f32),
                pltpu.SemaphoreType.DMA((NUM_MSGS,)),
                pltpu.SemaphoreType.DMA((NUM_MSGS,)),
                pltpu.SemaphoreType.DMA((NUM_SLOTS,)),
                pltpu.SemaphoreType.DMA((NUM_SLOTS,)),
                pltpu.SemaphoreType.DMA((PARTS, num_z)),
                pltpu.SemaphoreType.DMA((PARTS, num_z)),
                pltpu.SemaphoreType.DMA((2, red)),
                pltpu.SemaphoreType.DMA((2, red)),
                pltpu.SemaphoreType.DMA((RING,)),
                pltpu.SemaphoreType.DMA((RING,)),
                pltpu.SemaphoreType.DMA((7, num_z)),
                pltpu.SemaphoreType.DMA((7, num_z)),
                pltpu.SemaphoreType.DMA((2,)),
                pltpu.SemaphoreType.REGULAR,
                pltpu.SemaphoreType.REGULAR,
            ],
            compiler_params=pltpu.CompilerParams(
                collective_id=0, has_side_effects=True, vmem_limit_bytes=67043328),
        )(psi, left, right, w_flat)
        result = out.reshape(n_s, n_u, local_cols, full_rows).transpose(3, 0, 1, 2)
        return scal[0, 1:, 0, 0], scal[1, 1:, 0, 0], result

    return jax.shard_map(
        local_run, mesh=grid,
        in_specs=(P(('x', 'k'), None, None, ('z', 'y')), P(('x', 'k'), None, None), P(('z', 'y'), None, None), P()),
        out_specs=(P(), P(), P(('x', 'k'), None, None, ('z', 'y'))), check_vma=False)
```

time: 2340 us -> 577 us (0.25)
  waiting for transfers between devices: 1110 us -> 0 us
  blocking collectives: 869 us -> 0 us
  Pallas kernels: 0 us -> 560 us
  matrix products: 261 us -> 0 us
  other arithmetic: 28.7 us -> 4.05 us
    reduce_scatter x4 -> x0, waiting for transfers between devices: 992 us -> none  [apply_ham(): return lax.psum_scatter(part_out, 'col', scatter_dimension=3, tiled=True)]
    psum x9 -> x0, blocking collectives: 869 us -> none  [mean_dot(): return lax.psum(jnp.sum(left_vec * right_vec), ('col', 'row')) / num_elems]
    pallas_call x0 -> x1, Pallas kernels: none -> 560 us  [local_run(): pl.pallas_call(functools.partial(lanczos_kernel, float(psi_blk.size * gri...]
    dot_general x12 -> x0, matrix products: 261 us -> none  [the longest x4 139 us: apply_ham(): jnp.einsum('rctqb,bre->ctqe', stage_two, right_blk, precision=FULL_PREC,...]
    all_gather x4 -> x0, waiting for transfers between devices: 116 us -> none  [apply_ham(): gathered = lax.all_gather(vec_blk, 'row', axis=0, tiled=True)]
  transfers between devices with their start and end apart: 9 -> 0, of which waited for: 8 -> 0; matrix products, arithmetic and copies ran while one was open for 1% -> 0% of each run, Pallas kernels for 0% -> 0%
where the time goes in v2:
time: 577 us
  Pallas kernels  560 us (97%)
  local copies, waits for them, and re-layouts  12.1 us (2%)
    pallas_call x1, Pallas kernels, local_run(): pl.pallas_call(functools.partial(lanczos_kernel, float(psi_blk.size * gri...  560 us

profile of v2, /device:TPU:1, one launch (start us, length us, event | category | flops | bytes accessed | tf_op | source)
XLA Modules:
  0.0 577.0 jit_solution(12380339042729936404)
XLA Ops:
  0.6 1.0 copy.7
  1.6 0.4 copy.8
  2.0 0.1 mul.19
  2.1 0.1 copy.9
  2.2 4.0 broadcast_multiply_fusion
  6.3 7.2 %mul.23.w_ref = f32[360,360]{1,0:T(8,128)} reshape(f32[45,8,45,8]{3,2,1,0:T(8,128)} %broadcast_multiply_fusion) | data formatting | bytes 1036800 | tf_op jit(solution)/shard_map/mul | solution.py:518
  13.5 560.2 %shard_map.67 = (f32[9,64,256]{2,1,0:T(8,128)}, f32[2,5,8,128]{3,2,1,0:T(8,128)}) custom-call(f32[9,64,256]{2,1,0:T(8,128)} %bitcast.16, f32[5,256,2048]{2,1,0:T(8,128)} %bitcast.13, f32[5,64,2048]{2,1,0:T(8,128)} %bitcast.14, f32[360,360]{1,0:T(8,128)} %mul.23.w_ref), custom_call_target="tpu_custom_call" | custom-call | tf_op jit(solution)/shard_map/pallas_call | solution.py:522
  573.7 1.4 slice_reduce_fusion
  575.1 1.9 copy.11
  (1 shorter events, 0.0 us)

commit v3 on v0

v3 whole, which is shorter than its diff:
```python
import functools
import itertools

import jax
import jax.numpy as jnp
import numpy as np
from jax import lax
from jax.experimental import pallas as pl
from jax.experimental.pallas import tpu as pltpu
from jax.sharding import Mesh, PartitionSpec as P

LANCZOS_STEPS = 4
FULL_PREC = lax.Precision.HIGHEST
MESH_IDS = pl.DeviceIdType.MESH
scope = jax.named_scope
RING = 4
CORES = 2
PARTS = 4
STREAMS = 2
TREES = 4
BLOCKS = RING * RING
ALL_LINKS = [('x', 1), ('y', 1), ('x', -1), ('y', -1)]


def fine_mesh(mesh):
    shape = (mesh.shape['col'] // RING, RING, mesh.shape['row'] // CORES, CORES)
    return Mesh(mesh.devices.reshape(shape), ('z', 'y', 'x', 'k'))


def near(d):
    return min(d, RING - d)


def make_tree(turn):
    prefer = ALL_LINKS[turn:] + ALL_LINKS[:turn]
    load = dict.fromkeys(prefer, 0)
    tree = {}
    for offset in sorted(itertools.product(range(RING), repeat=2), key=lambda o: near(o[0]) + near(o[1])):
        options = [
            (axis, sign) for axis, d in zip('xy', offset) for sign in (-1, 1)
            if d and (-sign * d) % RING == near(d)]
        if options:
            tree[offset] = min(options, key=lambda link: (load[link], prefer.index(link)))
            load[tree[offset]] += 1
    return tree


def source_of(message):
    part, dx, dy = message
    axis, sign = LINKS[message]
    return (part, (dx + sign) % RING, dy) if axis == 'x' else (part, dx, (dy + sign) % RING)


LINKS = {(part, *offset): link for part in range(TREES) for offset, link in make_tree(part % len(ALL_LINKS)).items()}
SENDS = {}
for sent in LINKS:
    SENDS.setdefault(source_of(sent), []).append(sent)


def gather_order(release):
    free = dict.fromkeys(ALL_LINKS, 0.0)
    arrival = {}
    order = []

    def issue(now, message):
        order.append(message)
        for sent in SENDS.get(message, ()):
            link = LINKS[sent]
            free[link] = max(free[link], now) + 1.0
            arrival[sent] = free[link] + 0.6

    todo = [(now, (part, 0, 0)) for part, now in enumerate(release)]
    while len(order) < TREES * BLOCKS:
        left = [(now, message) for message, now in arrival.items() if message not in order]
        if todo and (not left or min(left)[0] > todo[0][0]):
            issue(*todo.pop(0))
        else:
            issue(*min(left))
    return order


def counts(*texts):
    return [int(c) for text in texts for c in text]


RELEASE = [0, 2.9000000000000004, 8.0, 8.0]
LAGS = counts('34456')
FINISH = [17, 25, 33, 72]
HOOKS = (7, 17, 43)
DURING_ONE = counts('113000051510220120300011340', '000000400000000000')
DURING_RING = counts('00000000000000000000000400020421')
DURING_TAIL = counts('10310200')
EARLY = sum(DURING_RING) + sum(DURING_TAIL)
HELD = gather_order(RELEASE)
INDEX = {message: i for i, message in enumerate(HELD)}
MESSAGES = [message for message in HELD if message in LINKS]
GROUP = TREES
WIDE = len(HELD) // 4
CHUNKS = [(c * WIDE, WIDE) for c in range(3)] + [(3 * WIDE + c * WIDE // 2, WIDE // 2) for c in range(2)]


def dot(lhs, rhs):
    return jnp.dot(lhs, rhs, precision=FULL_PREC, preferred_element_type=jnp.float32)


def lanczos_kernel(
        num_elems, num_z, psi_ref, left_ref, right_ref, mpo_ref, spread_out_ref, spread_in_ref, same_ref, out_ref, scal_ref,
        gath, right_full, left_own, left_turn, left_perm, w_mat, acc, mid, terms, ring, h_buf, v_buf, pack_out, pack_in,
        red_held, red_slots, alpha_sum,
        ag_send, ag_recv, sib_send, sib_recv, rs_send, rs_recv, red_send, red_recv, turn_send, turn_recv,
        env_send, env_recv, load_sem, ag_credit, rs_credit):
    phys, rows, cols = h_buf.shape[1:]
    bonds = right_full.shape[0]
    bonds_l = left_own.shape[0]
    piece = rows // TREES
    slab = rows // PARTS
    octs = rows // 8
    pairs = pack_in.shape[2]
    last_step = LANCZOS_STEPS - 1
    z, y, x, k = (lax.axis_index(name) for name in ('z', 'y', 'x', 'k'))
    other = 1 - k

    x_at, y_at = ([lax.rem(pos + d, RING) for d in range(RING)] for pos in (x, y))
    k_at = (k, other)

    def step_to(axis, sign):
        return {axis: {'x': x_at, 'y': y_at}[axis][sign % RING]}

    phases = (
        (num_z, z, lambda i: {'z': i}),
        (RING * RING * CORES, (x * CORES + k) * RING + y,
         lambda i: {'x': lax.div(i, CORES * RING), 'k': lax.rem(lax.div(i, RING), CORES), 'y': lax.rem(i, RING)}),
    )
    bases = (0, num_z)
    barrier = pltpu.get_barrier_semaphore()
    def repeat(lo, hi, fn):
        def body(i, c):
            fn(i)
            return c
        lax.fori_loop(lo, hi, body, 0)

    for count, me, device in phases:
        def enter(d, count=count, me=me, device=device):
            pl.semaphore_signal(barrier, inc=1, device_id=device(lax.rem(me + d, count)), device_id_type=MESH_IDS)
        repeat(1, count, enter)

    own_rows = pl.multiple_of(y * rows, rows)
    load_left = pltpu.make_async_copy(left_ref.at[:, pl.ds(own_rows, rows), :], left_own, load_sem.at[0])
    load_left.start()
    load_right = pltpu.make_async_copy(right_ref, right_full.at[:, pl.ds(own_rows, rows), :], load_sem.at[1])
    load_right.start()

    lane = lax.broadcasted_iota(jnp.int32, (rows, 128), 1)

    def pack(which, value):
        def body(pair):
            halves = [value(2 * pair), value(jnp.minimum(2 * pair + 1, phys - 1))]
            for target in range(RING):
                tile, half = divmod(target * rows, 128)
                first, second = (v[:, tile * 128:(tile + 1) * 128] for v in halves)
                if half == 0:
                    second = pltpu.roll(second, rows, 1)
                else:
                    first = pltpu.roll(first, rows, 1)
                pack_out[which, target, pair] = jnp.where(lane < rows, first, second)
        repeat(0, pairs, body)

    def turn_copy(which, src, dst, d, device):
        return pltpu.make_async_remote_copy(
            src_ref=pack_out.at[which, src], dst_ref=pack_in.at[which, dst],
            send_sem=turn_send.at[which, d], recv_sem=turn_recv.at[which, dst],
            device_id=device, device_id_type=MESH_IDS)

    def turn_start(which):
        for d in range(1, RING):
            peer = y_at[d]
            turn_copy(which, peer, y, d, {'y': peer}).start()
        pack_in[which, y] = pack_out[which, y]

    def turn_finish(which):
        for d in range(1, RING):
            peer = y_at[d]
            copy = turn_copy(which, peer, peer, d, {'y': peer})
            copy.wait_send()
            copy.wait_recv()

    def turned(which, pair):
        return jnp.concatenate([pack_in[which, i, pair] for i in range(RING)], axis=0)

    with scope('pack'):
        pack(0, lambda p: psi_ref[p])
    with scope('entry_barrier'):
        pl.semaphore_wait(barrier, sum(count - 1 for count, _, _ in phases))
    turn_start(0)
    h_buf[1] = jnp.zeros(h_buf.shape[1:], jnp.float32)
    v_buf[...] = jnp.zeros(v_buf.shape, jnp.float32)

    def sum_start(which, phase, value):
        count, me, device = phases[phase]
        red_held[which, phase] = value

        def send(d):
            pltpu.make_async_remote_copy(
                src_ref=red_held.at[which, phase], dst_ref=red_slots.at[which, bases[phase] + me],
                send_sem=red_send.at[which, bases[phase] + d], recv_sem=red_recv.at[which, bases[phase] + me],
                device_id=device(lax.rem(me + d, count)), device_id_type=MESH_IDS).start()
        repeat(1, count, send)
        red_slots[which, bases[phase] + me] = value

    def sum_finish(which, phase):
        count, me, device = phases[phase]

        def wait(d):
            peer = lax.rem(me + d, count)
            copy = pltpu.make_async_remote_copy(
                src_ref=red_held.at[which, phase], dst_ref=red_slots.at[which, bases[phase] + peer],
                send_sem=red_send.at[which, bases[phase] + d], recv_sem=red_recv.at[which, bases[phase] + peer],
                device_id=device(peer), device_id_type=MESH_IDS)
            copy.wait_send()
            copy.wait_recv()
        repeat(1, count, wait)
        return red_slots[which, bases[phase]:bases[phase] + count].sum(0)

    def mean_of(value):
        return jnp.broadcast_to(jnp.sum(value, axis=(0, 1), keepdims=True) * (1.0 / num_elems), (8, 128))

    def fold(values):
        lanes = values.reshape(-1, 8, cols).sum(0)
        tile = lanes[:, :128]
        for c in range(128, cols, 128):
            tile = tile + lanes[:, c:c + 128]
        return tile

    def gather_copy(message):
        index = INDEX[message]
        return pltpu.make_async_remote_copy(
            src_ref=gath.at[0, INDEX[source_of(message)]], dst_ref=gath.at[0, index],
            send_sem=ag_send.at[index], recv_sem=ag_recv.at[index],
            device_id=step_to(*LINKS[message]), device_id_type=MESH_IDS)

    def sibling_copy(index):
        span = pl.ds(index * GROUP, GROUP)
        return pltpu.make_async_remote_copy(
            src_ref=gath.at[0, span], dst_ref=gath.at[1, span],
            send_sem=sib_send.at[index], recv_sem=sib_recv.at[index],
            device_id={'k': other}, device_id_type=MESH_IDS)

    def groups_after(held, sequence):
        done = {}
        held = set(held)
        for message in sequence:
            held.add(message)
            for i in range(BLOCKS):
                group = HELD[i * GROUP:(i + 1) * GROUP]
                if message in group and held.issuperset(group):
                    done.setdefault(message, []).append(i)
        return done

    def take(message, groups):
        if message in LINKS:
            gather_copy(message).wait_recv()
        for sent in SENDS.get(message, ()):
            gather_copy(sent).start()
        for i in groups.get(message, ()):
            sibling_copy(i).start()

    def own_parts(s):
        each = TREES // PARTS
        return [(s * each + i, 0, 0) for i in range(each)]

    with scope('left'):
        load_left.wait()
    order = []
    for first, count in CHUNKS:
        order += [(dk, message) for dk in range(CORES) for message in HELD[first:first + count]]
    per_tile = 128 // piece
    lanes = lax.broadcasted_iota(jnp.int32, (rows, 128), 1)

    left_tiles = {
        (dx, dk, dy): pl.multiple_of(lax.div((x_at[dx] * CORES + k_at[dk]) * RING + y_at[dy], 2) * 128, 128)
        for dx in range(RING) for dk in range(CORES) for dy in range(RING)}

    def left_rows(l, c):
        for tile in range(left_own.shape[2] // 128):
            at = slice(tile * 128, (tile + 1) * 128)
            plain = left_own[l, :, at]
            rolled = pltpu.roll(plain, rows, 1)
            left_turn[0, :, at] = jnp.where(lax.rem(y, 2) == 0, plain, rolled)
            left_turn[1, :, at] = jnp.where(lax.rem(y, 2) == 0, rolled, plain)
        for tile in range(left_perm.shape[2] // 128):
            result = None
            for i in range(per_tile):
                dk, message = order[tile * per_tile + i]
                _, dx, dy = message
                values = left_turn[dy % 2, :, pl.ds(left_tiles[dx, dk, dy], 128)]
                if i != message[0]:
                    values = pltpu.roll(values, (i - message[0]) * piece % 128, 1)
                result = values if i == 0 else jnp.where(lanes >= i * piece, values, result)
            left_perm[l, :, tile * 128:(tile + 1) * 128] = result
        return c

    with scope('left_order'):
        lax.fori_loop(0, bonds_l, left_rows, 0)

    with scope('mpo'):
        wide = dot(dot(spread_out_ref[...], mpo_ref[...]), spread_in_ref[...])
        n_out, n_in = w_mat.shape
        same = jnp.broadcast_to(same_ref[...][None], (n_out // 8, 8, n_in)).reshape(n_out, n_in)
        w_mat[...] = wide * same

    with scope('turn_wait'):
        turn_finish(0)
    with scope('turn'):
        def unpack(pair):
            block = jnp.transpose(turned(0, pair))
            for i, p in enumerate((2 * pair, jnp.minimum(2 * pair + 1, phys - 1))):
                h_buf[0, p] = block[i * rows:(i + 1) * rows, :]
                for part in range(TREES):
                    span = slice(i * rows + part * piece, i * rows + (part + 1) * piece)
                    gath[0, INDEX[part, 0, 0], p] = block[span, :]
        repeat(0, pairs, unpack)
    own = [message for message in HELD if message not in LINKS]
    groups = groups_after((), own + MESSAGES[:EARLY])
    with scope('gather_early'):
        for message in own + MESSAGES[:EARLY]:
            take(message, groups)

    def stage_one(first, count, p, fresh):
        depth = count * piece
        rhs = jnp.concatenate(
            [gath[dk, pl.ds(first, count), p].reshape(depth, cols) for dk in range(CORES)], axis=0)
        column = pl.multiple_of(first * CORES * piece, 128)
        lhs = left_perm[:, :, pl.ds(column, CORES * depth)].reshape(bonds_l * rows, CORES * depth)
        res = dot(lhs, rhs).reshape(bonds_l, octs, 8, cols)
        acc[p] = jnp.where(fresh, 0.0, acc[p]) + res

    def at_steps(i, events):
        wide = 8
        for base in sorted({n // wide for n in events}):
            @pl.when(lax.div(i, wide) == base)
            def _(base=base):
                for n in range(base * wide, (base + 1) * wide):
                    if n in events:
                        @pl.when(i == n)
                        def _(n=n):
                            for event in events[n]:
                                event()

    half = rows // 2
    quarter = rows // 4

    def env_view(row, count, i):
        block = ring_block(0, i)
        return right_full.at[:, pl.ds(pl.multiple_of(row, 8), count), pl.ds(pl.multiple_of(block * cols, cols), cols)]

    def env_copy(kind, i, row, count, device):
        view = env_view(row, count, i)
        return pltpu.make_async_remote_copy(
            src_ref=view, dst_ref=view, send_sem=env_send.at[kind, i], recv_sem=env_recv.at[kind, i],
            device_id=device, device_id_type=MESH_IDS)

    up, down, far = y_at[1], y_at[3], y_at[2]

    def env_row(owner, core):
        return owner * rows + core * half

    def env_start(i):
        env_copy(0, i, env_row(y, k), half, {'y': up}).start()
        env_copy(1, i, env_row(y, k), half, {'y': down}).start()

    def env_pass(i):
        env_copy(0, i, env_row(down, k), half, {'y': up}).wait_recv()
        env_copy(2, i, env_row(down, k), quarter, {'y': up}).start()
        env_copy(4, i, env_row(down, k), half, {'k': other}).start()
        env_copy(1, i, env_row(up, k), half, {'y': down}).wait_recv()
        env_copy(3, i, env_row(up, k) + quarter, quarter, {'y': down}).start()
        env_copy(5, i, env_row(up, k), half, {'k': other}).start()

    def env_end(i):
        env_copy(2, i, env_row(far, k), quarter, {'y': up}).wait_recv()
        env_copy(3, i, env_row(far, k) + quarter, quarter, {'y': down}).wait_recv()
        env_copy(6, i, env_row(far, k), half, {'k': other}).start()

    def env_done(i):
        env_copy(4, i, env_row(down, other), half, {'k': other}).wait_recv()
        env_copy(5, i, env_row(up, other), half, {'k': other}).wait_recv()
        env_copy(6, i, env_row(far, other), half, {'k': other}).wait_recv()

    def env_sent(i):
        for kind, row, count in ((0, env_row(y, k), half), (1, env_row(y, k), half), (2, env_row(down, k), quarter),
                                 (3, env_row(up, k) + quarter, quarter), (4, env_row(down, k), half),
                                 (5, env_row(up, k), half), (6, env_row(far, k), half)):
            env_copy(kind, i, row, count, {'k': other}).wait_send()

    def env_ready(j, s, n):
        @pl.when((j == 0) & (s == 0))
        def _():
            with scope('env_ready'):
                @pl.when(n == 0)
                def _():
                    repeat(0, 2, env_pass)

                @pl.when(n + 2 < num_z)
                def _():
                    env_pass(n + 2)

                env_end(n)
                env_done(n)

    def way(s):
        return 1 - 2 * lax.rem(s, 2)

    def ring_side(s, n):
        return way(s) * (1 - 2 * lax.rem(n, 2))

    def ring_block(s, n):
        return lax.rem(z + num_z + ring_side(s, n) * (num_z // 2 - lax.div(n + 1, 2)), num_z)

    def ring_copy(src, s, n, h):
        return pltpu.make_async_remote_copy(
            src_ref=src, dst_ref=ring.at[s, n, h], send_sem=rs_send.at[s, n, h], recv_sem=rs_recv.at[s, n, h],
            device_id={'z': lax.rem(z + num_z + ring_side(s, n), num_z)}, device_id_type=MESH_IDS)

    def ring_wait(s, n, h):
        ring_copy(terms.at[s, n, h], s, n, h).wait_recv()

    def ring_pass(s, n, h):
        with scope('ring_pass'):
            ring_wait(s, n - 2, h)
            ring[s, n - 2, h] = ring[s, n - 2, h] + terms[s, n, h]
            ring_copy(ring.at[s, n - 2, h], s, n, h).start()

    def middle(o):
        res = dot(w_mat[...], acc[:, :, o].reshape(phys * bonds_l * 8, cols)).reshape(bonds, phys, 8, cols)
        for r in range(bonds):
            mid[:, o, :, r * cols:(r + 1) * cols] = res[r]

    def last_stage(s, n):
        lhs = mid[:, pl.ds(s * STREAMS, STREAMS)].reshape(phys * slab, bonds * cols)
        first = pl.multiple_of(ring_block(s, n) * cols, cols)
        rhs = right_full[:, :, pl.ds(first, cols)].reshape(bonds * cols, cols)
        res = dot(lhs, rhs).reshape(phys, STREAMS, 8, cols)
        for h in range(STREAMS):
            terms[s, n, h] = res[:, h]

    def new_direction(cur, alpha, beta_prev):
        nxt = 1 - cur
        a, b = alpha[0:1, 0:1], beta_prev[0:1, 0:1]
        def body(p, total):
            w = h_buf[cur, p] - a * v_buf[cur, p] - b * v_buf[nxt, p]
            v_buf[nxt, p] = w
            return total + fold(w * w)

        return lax.fori_loop(0, phys, body, jnp.zeros((8, 128), jnp.float32))

    def step(j, carry):
        alpha_part, beta_prev = carry
        cur = lax.rem(j, 2)
        nxt = 1 - cur
        more = j < last_step

        def alpha_z():
            sum_start(0, 1, sum_finish(0, 0))

        def alpha_plane():
            alpha = mean_of(sum_finish(0, 1))
            scal_ref[0, j] = alpha
            sum_start(1, 0, new_direction(cur, alpha, beta_prev))

        def beta_z():
            sum_start(1, 1, sum_finish(1, 0))

        sum_start(0, 0, alpha_part)
        queue = MESSAGES[EARLY:]
        groups = groups_after(own + MESSAGES[:EARLY], queue)
        wide_steps, all_steps = 3 * phys, 5 * phys
        events = {}
        hooks = dict(zip(HOOKS, (alpha_z, alpha_plane, beta_z)))
        for n, count in enumerate(DURING_ONE):
            at = events.setdefault(n * phys // 9, [])
            at += [functools.partial(take, message, groups) for message in queue[:count]]
            queue = queue[count:]
            if n % 9 == 0:
                first, count = CHUNKS[n // 9]
                at += [sibling_copy(i).wait_recv for i in range(first // GROUP, (first + count) // GROUP)]
            if n in hooks:
                at.append(hooks[n])

        def wide_step(i):
            with scope('events_wide'):
                at_steps(i, {n: e for n, e in events.items() if n < wide_steps})
            with scope('one_wide'):
                stage_one(lax.div(i, phys) * WIDE, WIDE, lax.rem(i, phys), i < phys)

        def half_step(i):
            with scope('events_half'):
                at_steps(i, {n - wide_steps: e for n, e in events.items() if n >= wide_steps})

            @pl.when((j == 0) & (i == phys))
            def _():
                load_right.wait()
                repeat(0, num_z, env_start)

            with scope('one_half'):
                stage_one(3 * WIDE + lax.div(i, phys) * (WIDE // 2), WIDE // 2, lax.rem(i, phys), i < 0)

        repeat(0, wide_steps, wide_step)
        repeat(0, all_steps - wide_steps, half_step)
        with scope('gather_sent'):
            for message in MESSAGES:
                gather_copy(message).wait_send()
            repeat(0, BLOCKS, lambda i: sibling_copy(i).wait_send())

        @pl.when(more)
        def _():
            for link in ALL_LINKS:
                pl.semaphore_signal(ag_credit, inc=1, device_id=step_to(*link), device_id_type=MESH_IDS)
            pl.semaphore_signal(ag_credit, inc=1, device_id={'k': other}, device_id_type=MESH_IDS)

        @pl.when(j > 0)
        def _():
            pl.semaphore_wait(rs_credit, 2)

        def scale():
            beta = jnp.sqrt(mean_of(sum_finish(1, 1)))
            scal_ref[1, j] = beta
            inv = (1.0 / beta)[0:1, 0:1]

            def normalize(p):
                v_buf[nxt, p] = v_buf[nxt, p] * inv
            repeat(0, phys, normalize)

            @pl.when(more)
            def _():
                pl.semaphore_wait(ag_credit, len(ALL_LINKS) + 1)

            @pl.when(j == last_step)
            def _():
                pack(1, lambda p: v_buf[nxt, p])
                turn_start(1)

        def finish(s):
            if s == 0:
                scale()
            with scope('ring_end'):
                for h in range(STREAMS):
                    for n in range(max(num_z - 3, 0), num_z - 1):
                        ring_wait(s, n, h)
            alpha, beta = scal_ref[0, j], scal_ref[1, j]
            a, b, inv = alpha[0:1, 0:1], beta_prev[0:1, 0:1], (1.0 / beta)[0:1, 0:1]
            span = slice(s * slab, (s + 1) * slab)

            def body(p, total):
                new = []
                for h in range(STREAMS):
                    at = slice(s * slab + 8 * h, s * slab + 8 * h + 8)
                    g_new = terms[s, num_z - 1, h, p]
                    for n in range(max(num_z - 3, 0), num_z - 1):
                        g_new = g_new + ring[s, n, h, p]
                    new.append((g_new - a * h_buf[cur, p, at, :] - b * h_buf[nxt, p, at, :]) * inv)
                h_new = jnp.concatenate(new, axis=0)
                h_buf[nxt, p, span, :] = h_new
                for i, message in enumerate(own_parts(s)):
                    gath[0, INDEX[message], p] = h_new[i * piece:(i + 1) * piece]
                return total + fold(v_buf[nxt, p, span, :] * h_new)

            total = lax.fori_loop(0, phys, body, jnp.zeros((8, 128), jnp.float32))
            alpha_sum[...] = total if s == 0 else alpha_sum[...] + total

            @pl.when(more)
            def _():
                for message in own_parts(s):
                    take(message, next_groups)

        def early(message):
            @pl.when(more)
            def _():
                take(message, next_groups)

        def happen(event):
            {'pass': ring_pass, 'finish': finish, 'early': early}[event[0]](*event[1:])

        ring_steps = PARTS * num_z
        events = {}
        for s in range(PARTS):
            for n in range(2, num_z - 1):
                at = s * num_z + n + LAGS[n - 2]
                events.setdefault(at, []).extend(('pass', s, n, h) for h in range(STREAMS))
            events.setdefault(FINISH[s] * num_z // 8, []).append(('finish', s))
        tail = [event for at in sorted(events) if at >= ring_steps for event in events.pop(at)]
        queue = MESSAGES[:EARLY]
        for at, count in enumerate(DURING_RING):
            events.setdefault(at * num_z // 8, []).extend(('early', message) for message in queue[:count])
            queue = queue[count:]
        mixed = []
        spare = list(DURING_TAIL)
        for i, event in enumerate(tail):
            mixed.append(event)
            count = len(queue) if i == len(tail) - 1 else spare.pop(0) if spare else 0
            mixed += [('early', message) for message in queue[:count]]
            queue = queue[count:]
        tail = mixed
        sequence = [event for at in sorted(events) for event in events[at]] + tail
        sequence = [
            message for kind, *what in sequence if kind != 'pass'
            for message in (own_parts(*what) if kind == 'finish' else what)]
        next_groups = groups_after((), sequence)

        def ring_step(i):
            s, n = lax.div(i, num_z), lax.rem(i, num_z)

            @pl.when(n == 0)
            def _():
                repeat(0, STREAMS, lambda o: middle(s * STREAMS + o))

            env_ready(j, s, n)
            with scope('last_stage'):
                last_stage(s, n)

            @pl.when(n < min(2, num_z - 1))
            def _():
                for h in range(STREAMS):
                    ring_copy(terms.at[s, n, h], s, n, h).start()

            with scope('events_ring'):
                at_steps(i, {at: [functools.partial(happen, event) for event in events[at]] for at in events})

        repeat(0, ring_steps, ring_step)
        with scope('tail'):
            for event in tail:
                happen(event)

        def ring_sent(i):
            s, n = lax.div(i, num_z - 1), lax.rem(i, num_z - 1)
            for h in range(STREAMS):
                ring_copy(terms.at[s, n, h], s, n, h).wait_send()
        repeat(0, PARTS * (num_z - 1), ring_sent)

        @pl.when(more)
        def _():
            for sign in (1, num_z - 1):
                pl.semaphore_signal(
                    rs_credit, inc=1, device_id={'z': lax.rem(z + sign, num_z)}, device_id_type=MESH_IDS)

        return alpha_sum[...], jnp.where(j > 0, scal_ref[1, j], 0.0)

    zero = jnp.zeros((8, 128), jnp.float32)
    _, beta_prev = lax.fori_loop(0, LANCZOS_STEPS, step, (zero, zero))
    repeat(0, num_z, env_sent)

    cur = LANCZOS_STEPS % 2
    shift = scal_ref[0, last_step][0:1, 0:1]
    b = beta_prev[0:1, 0:1]

    def end_body(p, sums):
        h, v = h_buf[cur, p], v_buf[cur, p]
        d = h - shift * v - b * v_buf[1 - cur, p]
        h_buf[1 - cur, p] = d
        return tuple(total + fold(term) for total, term in zip(sums, (v * h, d * d, d * v, v * v)))

    sums = lax.fori_loop(0, phys, end_body, (zero,) * 4)
    row = lax.broadcasted_iota(jnp.int32, (8, 128), 0)

    def squeeze(tile):
        tile = tile + pltpu.roll(tile, 4, 0)
        return tile + pltpu.roll(tile, 2, 0)

    packed = squeeze(sums[0])
    for i in range(1, 4):
        packed = jnp.where(row >= 2 * i, squeeze(sums[i]), packed)
    with scope('end_sum'):
        sum_start(0, 0, packed)
        pack(0, lambda p: h_buf[1 - cur, p])
        turn_start(0)
        sum_start(0, 1, sum_finish(0, 0))
        packed = sum_finish(0, 1)
    v_h, d_d, d_v, v_v = (mean_of(jnp.where((row >= 2 * i) & (row < 2 * i + 2), packed, 0.0)) for i in range(4))
    delta = v_h - shift
    beta = jnp.sqrt(d_d - 2.0 * delta * d_v + delta * delta * v_v)
    scal_ref[0, LANCZOS_STEPS] = v_h
    scal_ref[1, LANCZOS_STEPS] = beta
    inv = (1.0 / beta)[0:1, 0:1]
    delta = delta[0:1, 0:1]
    with scope('end_turn_wait'):
        turn_finish(1)
        turn_finish(0)
    with scope('end_turn'):
        def end_unpack(pair):
            block = jnp.transpose((turned(0, pair) - delta * turned(1, pair)) * inv)
            for i, p in enumerate((2 * pair, jnp.minimum(2 * pair + 1, phys - 1))):
                out_ref[p] = block[i * rows:(i + 1) * rows, :]
        repeat(0, pairs, end_unpack)


def solution(mesh):
    grid = fine_mesh(mesh)
    num_z = grid.shape['z']

    def local_run(psi_blk, left_blk, right_blk, mpo_pair):
        full_rows, n_s, n_u, local_cols = psi_blk.shape
        phys = n_s * n_u
        rows = full_rows // RING
        cols = local_cols * RING
        bonds_l, bonds_r = left_blk.shape[1], right_blk.shape[1]
        full_a, full_b = left_blk.shape[2], right_blk.shape[2]
        psi = psi_blk.transpose(1, 2, 3, 0).reshape(phys, local_cols, full_rows)
        left = left_blk.transpose(1, 0, 2)
        right = right_blk.transpose(1, 0, 2)
        mpo = mpo_pair.reshape(bonds_l, bonds_r, phys, phys).transpose(1, 3, 2, 0)
        mpo = mpo.reshape(bonds_r * phys, phys * bonds_l)
        eye = np.eye(8, dtype=np.float32)
        one = np.ones((1, 8), np.float32)
        spread_out = np.kron(np.eye(bonds_r * phys, dtype=np.float32), one.T)
        spread_in = np.kron(np.eye(phys * bonds_l, dtype=np.float32), one)
        same = np.tile(eye, (1, phys * bonds_l))
        red = num_z + RING * RING * CORES
        pairs = (phys + 1) // 2
        f32 = jnp.float32
        out, scal = pl.pallas_call(
            functools.partial(lanczos_kernel, float(psi_blk.size * grid.size), num_z),
            out_shape=(
                jax.ShapeDtypeStruct((phys, local_cols, full_rows), f32),
                jax.ShapeDtypeStruct((2, LANCZOS_STEPS + 1, 8, 128), f32),
            ),
            in_specs=[
                pl.BlockSpec(memory_space=pltpu.VMEM),
                pl.BlockSpec(memory_space=pl.ANY),
                pl.BlockSpec(memory_space=pl.ANY),
            ] + [pl.BlockSpec(memory_space=pltpu.VMEM)] * 4,
            out_specs=(pl.BlockSpec(memory_space=pltpu.VMEM), pl.BlockSpec(memory_space=pltpu.VMEM)),
            scratch_shapes=[
                pltpu.VMEM((CORES, len(HELD), phys, rows // TREES, cols), f32),
                pltpu.VMEM((bonds_r, cols, full_b), f32),
                pltpu.VMEM((bonds_l, rows, full_a), f32),
                pltpu.VMEM((2, rows, full_a), f32),
                pltpu.VMEM((bonds_l, rows, full_a), f32),
                pltpu.VMEM((bonds_r * phys * 8, phys * bonds_l * 8), f32),
                pltpu.VMEM((phys, bonds_l, rows // 8, 8, cols), f32),
                pltpu.VMEM((phys, rows // 8, 8, bonds_r * cols), f32),
                pltpu.VMEM((PARTS, num_z, STREAMS, phys, 8, cols), f32),
                pltpu.VMEM((PARTS, num_z - 1, STREAMS, phys, 8, cols), f32),
                pltpu.VMEM((2, phys, rows, cols), f32),
                pltpu.VMEM((2, phys, rows, cols), f32),
                pltpu.VMEM((2, RING, pairs, rows, 128), f32),
                pltpu.VMEM((2, RING, pairs, rows, 128), f32),
                pltpu.VMEM((2, 2, 8, 128), f32),
                pltpu.VMEM((2, red, 8, 128), f32),
                pltpu.VMEM((8, 128), f32),
                pltpu.SemaphoreType.DMA((len(HELD),)),
                pltpu.SemaphoreType.DMA((len(HELD),)),
                pltpu.SemaphoreType.DMA((BLOCKS,)),
                pltpu.SemaphoreType.DMA((BLOCKS,)),
                pltpu.SemaphoreType.DMA((PARTS, num_z - 1, STREAMS)),
                pltpu.SemaphoreType.DMA((PARTS, num_z - 1, STREAMS)),
                pltpu.SemaphoreType.DMA((2, red)),
                pltpu.SemaphoreType.DMA((2, red)),
                pltpu.SemaphoreType.DMA((2, RING)),
                pltpu.SemaphoreType.DMA((2, RING)),
                pltpu.SemaphoreType.DMA((7, num_z)),
                pltpu.SemaphoreType.DMA((7, num_z)),
                pltpu.SemaphoreType.DMA((2,)),
                pltpu.SemaphoreType.REGULAR,
                pltpu.SemaphoreType.REGULAR,
            ],
            compiler_params=pltpu.CompilerParams(
                collective_id=0, has_side_effects=True, vmem_limit_bytes=67043328),
        )(psi, left, right, mpo, spread_out, spread_in, same)
        result = out.reshape(n_s, n_u, local_cols, full_rows).transpose(3, 0, 1, 2)
        return scal[0, 1:, 0, 0], scal[1, 1:, 0, 0], result

    return jax.shard_map(
        local_run, mesh=grid,
        in_specs=(P(('x', 'k'), None, None, ('z', 'y')), P(('x', 'k'), None, None), P(('z', 'y'), None, None), P()),
        out_specs=(P(), P(), P(('x', 'k'), None, None, ('z', 'y'))), check_vma=False)
```

time: 2340 us -> 496 us (0.21)
  waiting for transfers between devices: 1110 us -> 0 us
  blocking collectives: 869 us -> 0 us
  Pallas kernels: 0 us -> 489 us
  matrix products: 261 us -> 0 us
  other arithmetic: 28.7 us -> 0 us
  local copies, waits for them, and re-layouts: 32.3 us -> 5.45 us
    reduce_scatter x4 -> x0, waiting for transfers between devices: 992 us -> none  [apply_ham(): return lax.psum_scatter(part_out, 'col', scatter_dimension=3, tiled=True)]
    psum x9 -> x0, blocking collectives: 869 us -> none  [mean_dot(): return lax.psum(jnp.sum(left_vec * right_vec), ('col', 'row')) / num_elems]
    pallas_call x0 -> x1, Pallas kernels: none -> 489 us  [local_run(): pl.pallas_call(functools.partial(lanczos_kernel, float(psi_blk.size * gri...]
    dot_general x12 -> x0, matrix products: 261 us -> none  [the longest x4 139 us: apply_ham(): jnp.einsum('rctqb,bre->ctqe', stage_two, right_blk, precision=FULL_PREC,...]
    all_gather x4 -> x0, waiting for transfers between devices: 116 us -> none  [apply_ham(): gathered = lax.all_gather(vec_blk, 'row', axis=0, tiled=True)]
  transfers between devices with their start and end apart: 9 -> 0, of which waited for: 8 -> 0; matrix products, arithmetic and copies ran while one was open for 1% -> 0% of each run, Pallas kernels for 0% -> 0%
where the time goes in v3:
time: 496 us; the launch traced here: 495 us
  Pallas kernels  489 us (99%)
  local copies, waits for them, and re-layouts  5.45 us (1%)
    pallas_call x1, Pallas kernels, local_run(): pl.pallas_call(functools.partial(lanczos_kernel, float(psi_blk.size * gri...  489 us

profile of v3, /device:TPU:1, one launch (start us, length us, event | category | flops | bytes accessed | tf_op | source)
XLA Modules:
  0.0 495.3 jit_solution(253562695061115028)
XLA Ops:
  0.6 1.0 copy.11
  1.6 0.4 copy.12
  2.0 0.1 reshape.20
  2.1 0.7 copy.13.mpo_ref
  2.8 489.2 %shard_map.94 = (f32[9,64,256]{2,1,0:T(8,128)}, f32[2,5,8,128]{3,2,1,0:T(8,128)}) custom-call(f32[9,64,256]{2,1,0:T(8,128)} %bitcast.17, f32[5,256,2048]{2,1,0:T(8,128)} %bitcast.13, f32[5,64,2048]{2,1,0:T(8,128)} %bitcast.14, f32[45,45]{1,0:T(8,128)} %copy.13.mpo_ref, f32[360,45]{1,0:T(8,128)} %constant.6.clone.spread_out_ref, ...), custom_call_target="tpu_custom_call" | custom-call | tf_op jit(solution)/shard_map/pallas_call | solution.py:719
  492.1 1.4 slice_reduce_fusion
  493.4 1.9 copy.15

commit v4 on v3

--- a/solution.py
+++ b/solution.py
@@ -13,6 +13,9 @@
 FULL_PREC = lax.Precision.HIGHEST
 MESH_IDS = pl.DeviceIdType.MESH
 scope = jax.named_scope
+SUB = 8
+LANES = 128
+TILE = (SUB, LANES)
 RING = 4
 CORES = 2
 PARTS = 4
@@ -83,14 +86,19 @@
     return [int(c) for text in texts for c in text]
 
 
-RELEASE = [0, 2.9000000000000004, 8.0, 8.0]
-LAGS = counts('34456')
-FINISH = [17, 25, 33, 72]
-HOOKS = (7, 17, 43)
-DURING_ONE = counts('113000051510220120300011340', '000000400000000000')
-DURING_RING = counts('00000000000000000000000400020421')
-DURING_TAIL = counts('10310200')
+RELEASE = [0, 3.9, 8.0, 10.0]
+LAGS = counts('22344')
+FINISH = [9, 14, 18, 32]
+HOOKS = (7, 15, 27)
+DURING_ONE = counts('000400102000130623103010210', '210200')
+DURING_RING = counts('0000000000040407')
+DURING_TAIL = counts('20020150')
 EARLY = sum(DURING_RING) + sum(DURING_TAIL)
+ENV_PIECES = 4
+ENV_STRIDE = 2
+ENV_STEPS = (1, 8, 14, 18, 23)
+CHUNK_STEPS = (0, 9, 18, 27, 30)
+SPAN = 4
 HELD = gather_order(RELEASE)
 INDEX = {message: i for i, message in enumerate(HELD)}
 MESSAGES = [message for message in HELD if message in LINKS]
@@ -147,17 +155,17 @@
     own_rows = pl.multiple_of(y * rows, rows)
     load_left = pltpu.make_async_copy(left_ref.at[:, pl.ds(own_rows, rows), :], left_own, load_sem.at[0])
     load_left.start()
-    load_right = pltpu.make_async_copy(right_ref, right_full.at[:, pl.ds(own_rows, rows), :], load_sem.at[1])
+    load_right = pltpu.make_async_copy(right_ref, right_full.at[:, pl.ds(y * RING, RING)], load_sem.at[1])
     load_right.start()
 
-    lane = lax.broadcasted_iota(jnp.int32, (rows, 128), 1)
+    lane = lax.broadcasted_iota(jnp.int32, (rows, LANES), 1)
 
     def pack(which, value):
         def body(pair):
             halves = [value(2 * pair), value(jnp.minimum(2 * pair + 1, phys - 1))]
             for target in range(RING):
-                tile, half = divmod(target * rows, 128)
-                first, second = (v[:, tile * 128:(tile + 1) * 128] for v in halves)
+                tile, half = divmod(target * rows, LANES)
+                first, second = (v[:, tile * LANES:(tile + 1) * LANES] for v in halves)
                 if half == 0:
                     second = pltpu.roll(second, rows, 1)
                 else:
@@ -222,13 +230,16 @@
         return red_slots[which, bases[phase]:bases[phase] + count].sum(0)
 
     def mean_of(value):
-        return jnp.broadcast_to(jnp.sum(value, axis=(0, 1), keepdims=True) * (1.0 / num_elems), (8, 128))
+        return jnp.broadcast_to(jnp.sum(value, axis=(0, 1), keepdims=True) * (1.0 / num_elems), TILE)
+
+    def only(tile):
+        return tile[:1, :1]
 
     def fold(values):
         lanes = values.reshape(-1, 8, cols).sum(0)
-        tile = lanes[:, :128]
-        for c in range(128, cols, 128):
-            tile = tile + lanes[:, c:c + 128]
+        tile = lanes[:, :LANES]
+        for c in range(LANES, cols, LANES):
+            tile = tile + lanes[:, c:c + LANES]
         return tile
 
     def gather_copy(message):
@@ -267,46 +278,6 @@
     def own_parts(s):
         each = TREES // PARTS
         return [(s * each + i, 0, 0) for i in range(each)]
-
-    with scope('left'):
-        load_left.wait()
-    order = []
-    for first, count in CHUNKS:
-        order += [(dk, message) for dk in range(CORES) for message in HELD[first:first + count]]
-    per_tile = 128 // piece
-    lanes = lax.broadcasted_iota(jnp.int32, (rows, 128), 1)
-
-    left_tiles = {
-        (dx, dk, dy): pl.multiple_of(lax.div((x_at[dx] * CORES + k_at[dk]) * RING + y_at[dy], 2) * 128, 128)
-        for dx in range(RING) for dk in range(CORES) for dy in range(RING)}
-
-    def left_rows(l, c):
-        for tile in range(left_own.shape[2] // 128):
-            at = slice(tile * 128, (tile + 1) * 128)
-            plain = left_own[l, :, at]
-            rolled = pltpu.roll(plain, rows, 1)
-            left_turn[0, :, at] = jnp.where(lax.rem(y, 2) == 0, plain, rolled)
-            left_turn[1, :, at] = jnp.where(lax.rem(y, 2) == 0, rolled, plain)
-        for tile in range(left_perm.shape[2] // 128):
-            result = None
-            for i in range(per_tile):
-                dk, message = order[tile * per_tile + i]
-                _, dx, dy = message
-                values = left_turn[dy % 2, :, pl.ds(left_tiles[dx, dk, dy], 128)]
-                if i != message[0]:
-                    values = pltpu.roll(values, (i - message[0]) * piece % 128, 1)
-                result = values if i == 0 else jnp.where(lanes >= i * piece, values, result)
-            left_perm[l, :, tile * 128:(tile + 1) * 128] = result
-        return c
-
-    with scope('left_order'):
-        lax.fori_loop(0, bonds_l, left_rows, 0)
-
-    with scope('mpo'):
-        wide = dot(dot(spread_out_ref[...], mpo_ref[...]), spread_in_ref[...])
-        n_out, n_in = w_mat.shape
-        same = jnp.broadcast_to(same_ref[...][None], (n_out // 8, 8, n_in)).reshape(n_out, n_in)
-        w_mat[...] = wide * same
 
     with scope('turn_wait'):
         turn_finish(0)
@@ -321,91 +292,135 @@
         repeat(0, pairs, unpack)
     own = [message for message in HELD if message not in LINKS]
     groups = groups_after((), own + MESSAGES[:EARLY])
+    for message in own:
+        take(message, groups)
+
+    with scope('left'):
+        load_left.wait()
+    order = []
+    for first, count in CHUNKS:
+        order += [(dk, message) for dk in range(CORES) for message in HELD[first:first + count]]
+    per_tile = LANES // piece
+    lanes = lax.broadcasted_iota(jnp.int32, (rows, LANES), 1)
+
+    left_tiles = {
+        (dx, dk, dy): pl.multiple_of(lax.div((x_at[dx] * CORES + k_at[dk]) * RING + y_at[dy], 2) * LANES, LANES)
+        for dx in range(RING) for dk in range(CORES) for dy in range(RING)}
+
+    def left_rows(l, c):
+        for tile in range(left_own.shape[2] // LANES):
+            at = slice(tile * LANES, (tile + 1) * LANES)
+            plain = left_own[l, :, at]
+            rolled = pltpu.roll(plain, rows, 1)
+            left_turn[0, :, at] = jnp.where(lax.rem(y, 2) == 0, plain, rolled)
+            left_turn[1, :, at] = jnp.where(lax.rem(y, 2) == 0, rolled, plain)
+        for tile in range(left_perm.shape[2] // LANES):
+            result = None
+            for i in range(per_tile):
+                dk, message = order[tile * per_tile + i]
+                _, dx, dy = message
+                values = left_turn[dy % 2, :, pl.ds(left_tiles[dx, dk, dy], LANES)]
+                if i != message[0]:
+                    values = pltpu.roll(values, (i - message[0]) * piece % LANES, 1)
+                result = values if i == 0 else jnp.where(lanes >= i * piece, values, result)
+            left_perm[l, :, tile * LANES:(tile + 1) * LANES] = result
+        return c
+
+    with scope('left_order'):
+        lax.fori_loop(0, bonds_l, left_rows, 0)
+
+    with scope('mpo'):
+        rows_out = lax.dot_general(
+            spread_out_ref[...], mpo_ref[...], (((1,), (1,)), ((), ())), precision=FULL_PREC,
+            preferred_element_type=jnp.float32)
+        wide = dot(rows_out, spread_in_ref[...])
+        n_out, n_in = w_mat.shape
+        same = jnp.broadcast_to(same_ref[...][None], (n_out // 8, 8, n_in)).reshape(n_out, n_in)
+        w_mat[...] = wide * same
+
     with scope('gather_early'):
-        for message in own + MESSAGES[:EARLY]:
+        for message in MESSAGES[:EARLY]:
             take(message, groups)
 
     def stage_one(first, count, p, fresh):
         depth = count * piece
         rhs = jnp.concatenate(
             [gath[dk, pl.ds(first, count), p].reshape(depth, cols) for dk in range(CORES)], axis=0)
-        column = pl.multiple_of(first * CORES * piece, 128)
+        column = pl.multiple_of(first * CORES * piece, LANES)
         lhs = left_perm[:, :, pl.ds(column, CORES * depth)].reshape(bonds_l * rows, CORES * depth)
         res = dot(lhs, rhs).reshape(bonds_l, octs, 8, cols)
         acc[p] = jnp.where(fresh, 0.0, acc[p]) + res
 
     def at_steps(i, events):
-        wide = 8
-        for base in sorted({n // wide for n in events}):
-            @pl.when(lax.div(i, wide) == base)
-            def _(base=base):
-                for n in range(base * wide, (base + 1) * wide):
-                    if n in events:
-                        @pl.when(i == n)
-                        def _(n=n):
-                            for event in events[n]:
-                                event()
-
-    half = rows // 2
-    quarter = rows // 4
-
-    def env_view(row, count, i):
-        block = ring_block(0, i)
-        return right_full.at[:, pl.ds(pl.multiple_of(row, 8), count), pl.ds(pl.multiple_of(block * cols, cols), cols)]
-
-    def env_copy(kind, i, row, count, device):
-        view = env_view(row, count, i)
+        steps = sorted(events)
+
+        def run(steps):
+            if len(steps) > 1:
+                middle = len(steps) // 2
+                lax.cond(i < steps[middle], lambda: run(steps[:middle]), lambda: run(steps[middle:]))
+            else:
+                for step in steps:
+                    @pl.when(i == step)
+                    def _():
+                        for event in events[step]:
+                            event()
+
+        run(steps)
+
+    up, down, far = y_at[1], y_at[3], y_at[2]
+    strip = right_full.shape[-1] // ENV_PIECES
+
+    def env_copy(kind, c, block, device, count=1, core=None):
+        span = pl.ds(c * strip, strip)
+        row = k if core is None else core
+        view = right_full.at[:, pl.ds(block, count), pl.ds(row, 1), :, span]
         return pltpu.make_async_remote_copy(
-            src_ref=view, dst_ref=view, send_sem=env_send.at[kind, i], recv_sem=env_recv.at[kind, i],
+            src_ref=view, dst_ref=view, send_sem=env_send.at[kind, c], recv_sem=env_recv.at[kind, c],
             device_id=device, device_id_type=MESH_IDS)
 
-    up, down, far = y_at[1], y_at[3], y_at[2]
-
-    def env_row(owner, core):
-        return owner * rows + core * half
-
-    def env_start(i):
-        env_copy(0, i, env_row(y, k), half, {'y': up}).start()
-        env_copy(1, i, env_row(y, k), half, {'y': down}).start()
-
-    def env_pass(i):
-        env_copy(0, i, env_row(down, k), half, {'y': up}).wait_recv()
-        env_copy(2, i, env_row(down, k), quarter, {'y': up}).start()
-        env_copy(4, i, env_row(down, k), half, {'k': other}).start()
-        env_copy(1, i, env_row(up, k), half, {'y': down}).wait_recv()
-        env_copy(3, i, env_row(up, k) + quarter, quarter, {'y': down}).start()
-        env_copy(5, i, env_row(up, k), half, {'k': other}).start()
-
-    def env_end(i):
-        env_copy(2, i, env_row(far, k), quarter, {'y': up}).wait_recv()
-        env_copy(3, i, env_row(far, k) + quarter, quarter, {'y': down}).wait_recv()
-        env_copy(6, i, env_row(far, k), half, {'k': other}).start()
-
-    def env_done(i):
-        env_copy(4, i, env_row(down, other), half, {'k': other}).wait_recv()
-        env_copy(5, i, env_row(up, other), half, {'k': other}).wait_recv()
-        env_copy(6, i, env_row(far, other), half, {'k': other}).wait_recv()
-
-    def env_sent(i):
-        for kind, row, count in ((0, env_row(y, k), half), (1, env_row(y, k), half), (2, env_row(down, k), quarter),
-                                 (3, env_row(up, k) + quarter, quarter), (4, env_row(down, k), half),
-                                 (5, env_row(up, k), half), (6, env_row(far, k), half)):
-            env_copy(kind, i, row, count, {'k': other}).wait_send()
-
-    def env_ready(j, s, n):
-        @pl.when((j == 0) & (s == 0))
-        def _():
-            with scope('env_ready'):
-                @pl.when(n == 0)
-                def _():
-                    repeat(0, 2, env_pass)
-
-                @pl.when(n + 2 < num_z)
-                def _():
-                    env_pass(n + 2)
-
-                env_end(n)
-                env_done(n)
+    def block_of(owner, d):
+        return owner * RING + x_at[d]
+
+    TAKEN = (0, 1)
+
+    def env_start(c):
+        for d in TAKEN:
+            env_copy(d, c, block_of(y, d), {'y': up}).start()
+            env_copy(2 + d, c, block_of(y, d), {'y': down}).start()
+
+    def env_pass_x(c, i, owner):
+        env_copy(6 + i, c, block_of(owner, 0), {'x': x_at[1]}).start()
+        env_copy(9 + i, c, block_of(owner, 1), {'x': x_at[3]}).start()
+
+    def env_pass(c):
+        for d in TAKEN:
+            env_copy(d, c, block_of(down, d), {'y': up}).wait_recv()
+            env_copy(2 + d, c, block_of(up, d), {'y': down}).wait_recv()
+        env_copy(4, c, block_of(down, 0), {'y': up}).start()
+        env_copy(5, c, block_of(up, 1), {'y': down}).start()
+        env_pass_x(c, 0, down)
+        env_pass_x(c, 1, up)
+
+    def env_far(c):
+        env_copy(4, c, block_of(far, 0), {'y': up}).wait_recv()
+        env_copy(5, c, block_of(far, 1), {'y': down}).wait_recv()
+        env_pass_x(c, 2, far)
+
+    def env_share(c):
+        for i, owner in enumerate((down, up, far)):
+            env_copy(6 + i, c, block_of(owner, 3), {'x': x_at[1]}).wait_recv()
+            env_copy(9 + i, c, block_of(owner, 2), {'x': x_at[3]}).wait_recv()
+            env_copy(12 + i, c, owner * RING, {'k': other}, RING).start()
+
+    def env_done(c):
+        for i, owner in enumerate((down, up, far)):
+            env_copy(12 + i, c, owner * RING, {'k': other}, RING, other).wait_recv()
+
+    def env_sent(c):
+        for kind in range(12):
+            env_copy(kind, c, 0, {'k': other}).wait_send()
+        for i in range(3):
+            env_copy(12 + i, c, 0, {'k': other}, RING).wait_send()
 
     def way(s):
         return 1 - 2 * lax.rem(s, 2)
@@ -435,23 +450,24 @@
         for r in range(bonds):
             mid[:, o, :, r * cols:(r + 1) * cols] = res[r]
 
-    def last_stage(s, n):
+    def last_stage(s, which):
         lhs = mid[:, pl.ds(s * STREAMS, STREAMS)].reshape(phys * slab, bonds * cols)
-        first = pl.multiple_of(ring_block(s, n) * cols, cols)
-        rhs = right_full[:, :, pl.ds(first, cols)].reshape(bonds * cols, cols)
-        res = dot(lhs, rhs).reshape(phys, STREAMS, 8, cols)
-        for h in range(STREAMS):
-            terms[s, n, h] = res[:, h]
+        for n in which:
+            first = pl.multiple_of(ring_block(s, n) * cols, cols)
+            rhs = right_full[:, :, :, :, pl.ds(first, cols)].reshape(bonds * cols, cols)
+            res = dot(lhs, rhs).reshape(phys, STREAMS, 8, cols)
+            for h in range(STREAMS):
+                terms[s, n, h] = res[:, h]
 
     def new_direction(cur, alpha, beta_prev):
         nxt = 1 - cur
-        a, b = alpha[0:1, 0:1], beta_prev[0:1, 0:1]
+        a, b = only(alpha), only(beta_prev)
         def body(p, total):
             w = h_buf[cur, p] - a * v_buf[cur, p] - b * v_buf[nxt, p]
             v_buf[nxt, p] = w
             return total + fold(w * w)
 
-        return lax.fori_loop(0, phys, body, jnp.zeros((8, 128), jnp.float32))
+        return lax.fori_loop(0, phys, body, jnp.zeros(TILE, jnp.float32))
 
     def step(j, carry):
         alpha_part, beta_prev = carry
@@ -470,21 +486,34 @@
         def beta_z():
             sum_start(1, 1, sum_finish(1, 0))
 
+        def in_first(event, *what):
+            @pl.when(j == 0)
+            def _():
+                event(*what)
+
         sum_start(0, 0, alpha_part)
         queue = MESSAGES[EARLY:]
         groups = groups_after(own + MESSAGES[:EARLY], queue)
-        wide_steps, all_steps = 3 * phys, 5 * phys
+        wide_steps = 3 * phys
+        each = 3 if phys % 3 == 0 else 1
+        half_steps = 2 * phys // each
         events = {}
         hooks = dict(zip(HOOKS, (alpha_z, alpha_plane, beta_z)))
         for n, count in enumerate(DURING_ONE):
-            at = events.setdefault(n * phys // 9, [])
+            at = n * phys // 9 if n < 27 else wide_steps + (n - 27) * half_steps // 6
+            at = events.setdefault(at, [])
             at += [functools.partial(take, message, groups) for message in queue[:count]]
             queue = queue[count:]
-            if n % 9 == 0:
-                first, count = CHUNKS[n // 9]
+            if n in CHUNK_STEPS:
+                first, count = CHUNKS[CHUNK_STEPS.index(n)]
                 at += [sibling_copy(i).wait_recv for i in range(first // GROUP, (first + count) // GROUP)]
             if n in hooks:
                 at.append(hooks[n])
+            for event in (load_right.wait,) * (n == ENV_STEPS[0]):
+                at.append(functools.partial(in_first, event))
+            for first_step, event in zip(ENV_STEPS, (env_start, env_pass, env_far, env_share, env_done)):
+                if 0 <= n - first_step < ENV_PIECES * ENV_STRIDE and (n - first_step) % ENV_STRIDE == 0:
+                    at.append(functools.partial(in_first, event, (n - first_step) // ENV_STRIDE))
 
         def wide_step(i):
             with scope('events_wide'):
@@ -496,16 +525,13 @@
             with scope('events_half'):
                 at_steps(i, {n - wide_steps: e for n, e in events.items() if n >= wide_steps})
 
-            @pl.when((j == 0) & (i == phys))
-            def _():
-                load_right.wait()
-                repeat(0, num_z, env_start)
-
             with scope('one_half'):
-                stage_one(3 * WIDE + lax.div(i, phys) * (WIDE // 2), WIDE // 2, lax.rem(i, phys), i < 0)
+                chunk, p = lax.div(i * each, phys), lax.rem(i * each, phys)
+                for q in range(each):
+                    stage_one(3 * WIDE + chunk * (WIDE // 2), WIDE // 2, p + q, i < 0)
 
         repeat(0, wide_steps, wide_step)
-        repeat(0, all_steps - wide_steps, half_step)
+        repeat(0, half_steps, half_step)
         with scope('gather_sent'):
             for message in MESSAGES:
                 gather_copy(message).wait_send()
@@ -524,7 +550,7 @@
         def scale():
             beta = jnp.sqrt(mean_of(sum_finish(1, 1)))
             scal_ref[1, j] = beta
-            inv = (1.0 / beta)[0:1, 0:1]
+            inv = only(1.0 / beta)
 
             def normalize(p):
                 v_buf[nxt, p] = v_buf[nxt, p] * inv
@@ -547,7 +573,7 @@
                     for n in range(max(num_z - 3, 0), num_z - 1):
                         ring_wait(s, n, h)
             alpha, beta = scal_ref[0, j], scal_ref[1, j]
-            a, b, inv = alpha[0:1, 0:1], beta_prev[0:1, 0:1], (1.0 / beta)[0:1, 0:1]
+            a, b, inv = only(alpha), only(beta_prev), only(1.0 / beta)
             span = slice(s * slab, (s + 1) * slab)
 
             def body(p, total):
@@ -564,7 +590,7 @@
                     gath[0, INDEX[message], p] = h_new[i * piece:(i + 1) * piece]
                 return total + fold(v_buf[nxt, p, span, :] * h_new)
 
-            total = lax.fori_loop(0, phys, body, jnp.zeros((8, 128), jnp.float32))
+            total = lax.fori_loop(0, phys, body, jnp.zeros(TILE, jnp.float32))
             alpha_sum[...] = total if s == 0 else alpha_sum[...] + total
 
             @pl.when(more)
@@ -580,17 +606,18 @@
         def happen(event):
             {'pass': ring_pass, 'finish': finish, 'early': early}[event[0]](*event[1:])
 
-        ring_steps = PARTS * num_z
+        pairs_z = num_z // 2
+        ring_steps = PARTS * pairs_z
         events = {}
         for s in range(PARTS):
             for n in range(2, num_z - 1):
-                at = s * num_z + n + LAGS[n - 2]
+                at = s * pairs_z + n // 2 + LAGS[n - 2]
                 events.setdefault(at, []).extend(('pass', s, n, h) for h in range(STREAMS))
-            events.setdefault(FINISH[s] * num_z // 8, []).append(('finish', s))
+            events.setdefault(FINISH[s] * pairs_z // SPAN, []).append(('finish', s))
         tail = [event for at in sorted(events) if at >= ring_steps for event in events.pop(at)]
         queue = MESSAGES[:EARLY]
         for at, count in enumerate(DURING_RING):
-            events.setdefault(at * num_z // 8, []).extend(('early', message) for message in queue[:count])
+            events.setdefault(at * pairs_z // SPAN, []).extend(('early', message) for message in queue[:count])
             queue = queue[count:]
         mixed = []
         spare = list(DURING_TAIL)
@@ -607,20 +634,22 @@
         next_groups = groups_after((), sequence)
 
         def ring_step(i):
-            s, n = lax.div(i, num_z), lax.rem(i, num_z)
-
-            @pl.when(n == 0)
+            s, t = lax.div(i, pairs_z), lax.rem(i, pairs_z)
+
+            @pl.when(t == 0)
             def _():
-                repeat(0, STREAMS, lambda o: middle(s * STREAMS + o))
-
-            env_ready(j, s, n)
+                with scope('middle'):
+                    for o in range(STREAMS):
+                        middle(s * STREAMS + o)
+
             with scope('last_stage'):
-                last_stage(s, n)
-
-            @pl.when(n < min(2, num_z - 1))
+                last_stage(s, (2 * t, 2 * t + 1))
+
+            @pl.when(t == 0)
             def _():
-                for h in range(STREAMS):
-                    ring_copy(terms.at[s, n, h], s, n, h).start()
+                for n in range(min(2, num_z - 1)):
+                    for h in range(STREAMS):
+                        ring_copy(terms.at[s, n, h], s, n, h).start()
 
             with scope('events_ring'):
                 at_steps(i, {at: [functools.partial(happen, event) for event in events[at]] for at in events})
@@ -644,13 +673,13 @@
 
         return alpha_sum[...], jnp.where(j > 0, scal_ref[1, j], 0.0)
 
-    zero = jnp.zeros((8, 128), jnp.float32)
+    zero = jnp.zeros(TILE, jnp.float32)
     _, beta_prev = lax.fori_loop(0, LANCZOS_STEPS, step, (zero, zero))
-    repeat(0, num_z, env_sent)
+    repeat(0, ENV_PIECES, env_sent)
 
     cur = LANCZOS_STEPS % 2
-    shift = scal_ref[0, last_step][0:1, 0:1]
-    b = beta_prev[0:1, 0:1]
+    shift = only(scal_ref[0, last_step])
+    b = only(beta_prev)
 
     def end_body(p, sums):
         h, v = h_buf[cur, p], v_buf[cur, p]
@@ -659,7 +688,7 @@
         return tuple(total + fold(term) for total, term in zip(sums, (v * h, d * d, d * v, v * v)))
 
     sums = lax.fori_loop(0, phys, end_body, (zero,) * 4)
-    row = lax.broadcasted_iota(jnp.int32, (8, 128), 0)
+    row = lax.broadcasted_iota(jnp.int32, TILE, 0)
 
     def squeeze(tile):
         tile = tile + pltpu.roll(tile, 4, 0)
@@ -679,8 +708,8 @@
     beta = jnp.sqrt(d_d - 2.0 * delta * d_v + delta * delta * v_v)
     scal_ref[0, LANCZOS_STEPS] = v_h
     scal_ref[1, LANCZOS_STEPS] = beta
-    inv = (1.0 / beta)[0:1, 0:1]
-    delta = delta[0:1, 0:1]
+    inv = only(1.0 / beta)
+    delta = only(delta)
     with scope('end_turn_wait'):
         turn_finish(1)
         turn_finish(0)
@@ -705,13 +734,14 @@
         full_a, full_b = left_blk.shape[2], right_blk.shape[2]
         psi = psi_blk.transpose(1, 2, 3, 0).reshape(phys, local_cols, full_rows)
         left = left_blk.transpose(1, 0, 2)
-        right = right_blk.transpose(1, 0, 2)
-        mpo = mpo_pair.reshape(bonds_l, bonds_r, phys, phys).transpose(1, 3, 2, 0)
-        mpo = mpo.reshape(bonds_r * phys, phys * bonds_l)
+        right = right_blk.transpose(1, 0, 2).reshape(bonds_r, RING, CORES, 8, full_b)
+        mpo = mpo_pair.transpose(0, 2, 3, 4, 5, 1).reshape(bonds_l * phys, phys * bonds_r)
         eye = np.eye(8, dtype=np.float32)
         one = np.ones((1, 8), np.float32)
-        spread_out = np.kron(np.eye(bonds_r * phys, dtype=np.float32), one.T)
-        spread_in = np.kron(np.eye(phys * bonds_l, dtype=np.float32), one)
+        order_out = np.arange(phys * bonds_r).reshape(phys, bonds_r).T.ravel()
+        order_in = np.arange(bonds_l * phys).reshape(bonds_l, phys).T.ravel()
+        spread_out = np.kron(np.eye(order_out.size, dtype=np.float32)[order_out], one.T)
+        spread_in = np.kron(np.eye(order_in.size, dtype=np.float32)[:, order_in], one)
         same = np.tile(eye, (1, phys * bonds_l))
         red = num_z + RING * RING * CORES
         pairs = (phys + 1) // 2
@@ -720,7 +750,7 @@
             functools.partial(lanczos_kernel, float(psi_blk.size * grid.size), num_z),
             out_shape=(
                 jax.ShapeDtypeStruct((phys, local_cols, full_rows), f32),
-                jax.ShapeDtypeStruct((2, LANCZOS_STEPS + 1, 8, 128), f32),
+                jax.ShapeDtypeStruct((2, LANCZOS_STEPS + 1) + TILE, f32),
             ),
             in_specs=[
                 pl.BlockSpec(memory_space=pltpu.VMEM),
@@ -730,7 +760,7 @@
             out_specs=(pl.BlockSpec(memory_space=pltpu.VMEM), pl.BlockSpec(memory_space=pltpu.VMEM)),
             scratch_shapes=[
                 pltpu.VMEM((CORES, len(HELD), phys, rows // TREES, cols), f32),
-                pltpu.VMEM((bonds_r, cols, full_b), f32),
+                pltpu.VMEM((bonds_r, BLOCKS, CORES, 8, full_b), f32),
                 pltpu.VMEM((bonds_l, rows, full_a), f32),
                 pltpu.VMEM((2, rows, full_a), f32),
                 pltpu.VMEM((bonds_l, rows, full_a), f32),
@@ -741,11 +771,11 @@
                 pltpu.VMEM((PARTS, num_z - 1, STREAMS, phys, 8, cols), f32),
                 pltpu.VMEM((2, phys, rows, cols), f32),
                 pltpu.VMEM((2, phys, rows, cols), f32),
-                pltpu.VMEM((2, RING, pairs, rows, 128), f32),
-                pltpu.VMEM((2, RING, pairs, rows, 128), f32),
-                pltpu.VMEM((2, 2, 8, 128), f32),
-                pltpu.VMEM((2, red, 8, 128), f32),
-                pltpu.VMEM((8, 128), f32),
+                pltpu.VMEM((2, RING, pairs, rows, LANES), f32),
+                pltpu.VMEM((2, RING, pairs, rows, LANES), f32),
+                pltpu.VMEM((2, 2) + TILE, f32),
+                pltpu.VMEM((2, red) + TILE, f32),
+                pltpu.VMEM(TILE, f32),
                 pltpu.SemaphoreType.DMA((len(HELD),)),
                 pltpu.SemaphoreType.DMA((len(HELD),)),
                 pltpu.SemaphoreType.DMA((BLOCKS,)),
@@ -756,8 +786,8 @@
                 pltpu.SemaphoreType.DMA((2, red)),
                 pltpu.SemaphoreType.DMA((2, RING)),
                 pltpu.SemaphoreType.DMA((2, RING)),
-                pltpu.SemaphoreType.DMA((7, num_z)),
-                pltpu.SemaphoreType.DMA((7, num_z)),
+                pltpu.SemaphoreType.DMA((15, ENV_PIECES)),
+                pltpu.SemaphoreType.DMA((15, ENV_PIECES)),
                 pltpu.SemaphoreType.DMA((2,)),
                 pltpu.SemaphoreType.REGULAR,
                 pltpu.SemaphoreType.REGULAR,

time: 496 us -> 479 us (0.966)
  Pallas kernels: 489 us -> 473 us
    pallas_call x1, Pallas kernels: 489 us -> 473 us  [local_run(): pl.pallas_call(functools.partial(lanczos_kernel, float(psi_blk.size * gri...]
where the time goes in v4:
time: 479 us
  Pallas kernels  473 us (99%)
  local copies, waits for them, and re-layouts  5 us (1%)
    pallas_call x1, Pallas kernels, local_run(): pl.pallas_call(functools.partial(lanczos_kernel, float(psi_blk.size * gri...  473 us

profile of v4, /device:TPU:1, one launch (start us, length us, event | category | flops | bytes accessed | tf_op | source)
XLA Modules:
  0.0 479.0 jit_solution(1454941070321621644)
XLA Ops:
  0.6 1.7 reshape.20.mpo_ref
  2.4 473.4 %shard_map.94 = (f32[9,64,256]{2,1,0:T(8,128)}, f32[2,5,8,128]{3,2,1,0:T(8,128)}) custom-call(f32[9,64,256]{2,1,0:T(8,128)} %bitcast.14, f32[5,256,2048]{2,1,0:T(8,128)} %bitcast.11, f32[5,4,2,8,2048]{4,3,2,1,0:T(8,128)} %bitcast.12, f32[45,45]{1,0:T(8,128)} %reshape.20.mpo_ref, f32[360,45]{1,0:T(8,128)} %constant.6.clone.spread_out_ref, ...), custom_call_target="tpu_custom_call" | custom-call | tf_op jit(solution)/shard_map/pallas_call | solution.py:749
  475.7 1.4 slice_reduce_fusion
  477.1 1.9 copy.11

commit v5 on v4

--- a/solution.py
+++ b/solution.py
@@ -86,17 +86,18 @@
     return [int(c) for text in texts for c in text]
 
 
-RELEASE = [0, 3.9, 8.0, 10.0]
-LAGS = counts('22344')
-FINISH = [9, 14, 18, 32]
-HOOKS = (7, 15, 27)
-DURING_ONE = counts('000400102000130623103010210', '210200')
-DURING_RING = counts('0000000000040407')
-DURING_TAIL = counts('20020150')
+RELEASE = [0, 2.9, 3.5, 5.5]
+PAIR_ORDER = counts('0101202101323332')
+LAGS = (counts('11021'), counts('16253'), counts('14130'), counts('02445'))
+FINISH = [11, 15, 28, 29]
+HOOKS = (1, 11, 16)
+DURING_ONE = counts('113202510123420221111120300', '011200')
+DURING_RING = counts('0000000000000311')
+DURING_TAIL = counts('07002100')
 EARLY = sum(DURING_RING) + sum(DURING_TAIL)
 ENV_PIECES = 4
-ENV_STRIDE = 2
-ENV_STEPS = (1, 8, 14, 18, 23)
+ENV_STRIDE = 3
+ENV_STEPS = (0, 6, 14, 15, 22)
 CHUNK_STEPS = (0, 9, 18, 27, 30)
 SPAN = 4
 HELD = gather_order(RELEASE)
@@ -504,16 +505,16 @@
             at = events.setdefault(at, [])
             at += [functools.partial(take, message, groups) for message in queue[:count]]
             queue = queue[count:]
+            for event in (load_right.wait,) * (n == ENV_STEPS[0]):
+                at.append(functools.partial(in_first, event))
+            for first_step, event in zip(ENV_STEPS, (env_start, env_pass, env_far, env_share, env_done)):
+                if 0 <= n - first_step < ENV_PIECES * ENV_STRIDE and (n - first_step) % ENV_STRIDE == 0:
+                    at.append(functools.partial(in_first, event, (n - first_step) // ENV_STRIDE))
             if n in CHUNK_STEPS:
                 first, count = CHUNKS[CHUNK_STEPS.index(n)]
                 at += [sibling_copy(i).wait_recv for i in range(first // GROUP, (first + count) // GROUP)]
             if n in hooks:
                 at.append(hooks[n])
-            for event in (load_right.wait,) * (n == ENV_STEPS[0]):
-                at.append(functools.partial(in_first, event))
-            for first_step, event in zip(ENV_STEPS, (env_start, env_pass, env_far, env_share, env_done)):
-                if 0 <= n - first_step < ENV_PIECES * ENV_STRIDE and (n - first_step) % ENV_STRIDE == 0:
-                    at.append(functools.partial(in_first, event, (n - first_step) // ENV_STRIDE))
 
         def wide_step(i):
             with scope('events_wide'):
@@ -608,10 +609,15 @@
 
         pairs_z = num_z // 2
         ring_steps = PARTS * pairs_z
+        pairs_at = []
+        for s in PAIR_ORDER:
+            if sum(s == other_s for other_s, _ in pairs_at) < pairs_z:
+                pairs_at.append((s, sum(s == other_s for other_s, _ in pairs_at)))
+        slots = {pair: i for i, pair in enumerate(pairs_at)}
         events = {}
         for s in range(PARTS):
             for n in range(2, num_z - 1):
-                at = s * pairs_z + n // 2 + LAGS[n - 2]
+                at = slots[s, n // 2] + LAGS[s][n - 2]
                 events.setdefault(at, []).extend(('pass', s, n, h) for h in range(STREAMS))
             events.setdefault(FINISH[s] * pairs_z // SPAN, []).append(('finish', s))
         tail = [event for at in sorted(events) if at >= ring_steps for event in events.pop(at)]
@@ -634,7 +640,9 @@
         next_groups = groups_after((), sequence)
 
         def ring_step(i):
-            s, t = lax.div(i, pairs_z), lax.rem(i, pairs_z)
+            s, t = pairs_at[0]
+            for n, pair in enumerate(pairs_at):
+                s, t = jnp.where(i == n, pair[0], s), jnp.where(i == n, pair[1], t)
 
             @pl.when(t == 0)
             def _():

time: 479 us -> 465 us (0.971)
  Pallas kernels: 473 us -> 460 us
    pallas_call x1, Pallas kernels: 473 us -> 460 us  [local_run(): pl.pallas_call(functools.partial(lanczos_kernel, float(psi_blk.size * gri...]
where the time goes in v5:
time: 465 us
  Pallas kernels  460 us (99%)
  local copies, waits for them, and re-layouts  5 us (1%)
    pallas_call x1, Pallas kernels, local_run(): pl.pallas_call(functools.partial(lanczos_kernel, float(psi_blk.size * gri...  460 us

profile of v5, /device:TPU:1, one launch (start us, length us, event | category | flops | bytes accessed | tf_op | source)
XLA Modules:
  0.0 465.2 jit_solution(13528199819873598649)
XLA Ops:
  0.6 1.7 reshape.20.mpo_ref
  2.4 459.5 %shard_map.94 = (f32[9,64,256]{2,1,0:T(8,128)}, f32[2,5,8,128]{3,2,1,0:T(8,128)}) custom-call(f32[9,64,256]{2,1,0:T(8,128)} %bitcast.14, f32[5,256,2048]{2,1,0:T(8,128)} %bitcast.11, f32[5,4,2,8,2048]{4,3,2,1,0:T(8,128)} %bitcast.12, f32[45,45]{1,0:T(8,128)} %reshape.20.mpo_ref, f32[360,45]{1,0:T(8,128)} %constant.6.clone.spread_out_ref, ...), custom_call_target="tpu_custom_call" | custom-call | tf_op jit(solution)/shard_map/pallas_call | solution.py:757
  461.9 1.4 slice_reduce_fusion
  463.3 1.9 copy.11

commit v6 on v5

--- a/solution.py
+++ b/solution.py
@@ -83,21 +83,21 @@
 
 
 def counts(*texts):
-    return [int(c) for text in texts for c in text]
-
-
-RELEASE = [0, 2.9, 3.5, 5.5]
-PAIR_ORDER = counts('0101202101323332')
-LAGS = (counts('11021'), counts('16253'), counts('14130'), counts('02445'))
-FINISH = [11, 15, 28, 29]
-HOOKS = (1, 11, 16)
-DURING_ONE = counts('113202510123420221111120300', '011200')
-DURING_RING = counts('0000000000000311')
-DURING_TAIL = counts('07002100')
+    return [int(c, 36) for text in texts for c in text]
+
+
+RELEASE = [0, 2.9, 4.5, 8.0]
+PAIR_ORDER = counts('0101220013132323')
+LAGS = (counts('11011'), counts('35040'), counts('39276'), counts('17387'))
+FINISH = [9, 17, 23, 24]
+HOOKS = (7, 15, 30)
+DURING_ONE = counts('500020104111105222303030100', '301300')
+DURING_RING = counts('0000000000000400')
+DURING_TAIL = counts('000102004010301')
 EARLY = sum(DURING_RING) + sum(DURING_TAIL)
-ENV_PIECES = 4
-ENV_STRIDE = 3
-ENV_STEPS = (0, 6, 14, 15, 22)
+ENV_STEPS = (counts('g515i4mp'), counts('sa2btbvw'), counts('wh8kwrww'), counts('wkbnwtxw'), counts('xontywyx'))
+ENV_PIECES = len(ENV_STEPS[0])
+ENV_LEAD = 2
 CHUNK_STEPS = (0, 9, 18, 27, 30)
 SPAN = 4
 HELD = gather_order(RELEASE)
@@ -201,6 +201,71 @@
     with scope('entry_barrier'):
         pl.semaphore_wait(barrier, sum(count - 1 for count, _, _ in phases))
     turn_start(0)
+
+    up, down, far = y_at[1], y_at[3], y_at[2]
+    strip = right_full.shape[-1] // ENV_PIECES
+
+    def env_copy(kind, c, block, device, count=1, core=None):
+        span = pl.ds(c * strip, strip)
+        row = k if core is None else core
+        view = right_full.at[:, pl.ds(block, count), pl.ds(row, 1), :, span]
+        return pltpu.make_async_remote_copy(
+            src_ref=view, dst_ref=view, send_sem=env_send.at[kind, c], recv_sem=env_recv.at[kind, c],
+            device_id=device, device_id_type=MESH_IDS)
+
+    def block_of(owner, d):
+        return owner * RING + x_at[d]
+
+    TAKEN = (0, 1)
+
+    def env_start(c):
+        for d in TAKEN:
+            env_copy(d, c, block_of(y, d), {'y': up}).start()
+            env_copy(2 + d, c, block_of(y, d), {'y': down}).start()
+
+    def env_pass_x(c, i, owner):
+        env_copy(6 + i, c, block_of(owner, 0), {'x': x_at[1]}).start()
+        env_copy(9 + i, c, block_of(owner, 1), {'x': x_at[3]}).start()
+
+    def env_pass(c):
+        for d in TAKEN:
+            env_copy(d, c, block_of(down, d), {'y': up}).wait_recv()
+            env_copy(2 + d, c, block_of(up, d), {'y': down}).wait_recv()
+        env_copy(4, c, block_of(down, 0), {'y': up}).start()
+        env_copy(5, c, block_of(up, 1), {'y': down}).start()
+        env_pass_x(c, 0, down)
+        env_pass_x(c, 1, up)
+
+    def env_far(c):
+        env_copy(4, c, block_of(far, 0), {'y': up}).wait_recv()
+        env_copy(5, c, block_of(far, 1), {'y': down}).wait_recv()
+        env_pass_x(c, 2, far)
+
+    def env_share(c):
+        for i, owner in enumerate((down, up, far)):
+            env_copy(6 + i, c, block_of(owner, 3), {'x': x_at[1]}).wait_recv()
+            env_copy(9 + i, c, block_of(owner, 2), {'x': x_at[3]}).wait_recv()
+            env_copy(12 + i, c, owner * RING, {'k': other}, RING).start()
+
+    def env_done(c):
+        for i, owner in enumerate((down, up, far)):
+            env_copy(12 + i, c, owner * RING, {'k': other}, RING, other).wait_recv()
+
+    env_events = (env_start, env_pass, env_far, env_share, env_done)
+
+    def env_before(step):
+        for c in range(ENV_PIECES):
+            if ENV_STEPS[0][c] == step:
+                env_start(c)
+
+    def env_sent(c):
+        for kind in range(12):
+            env_copy(kind, c, 0, {'k': other}).wait_send()
+        for i in range(3):
+            env_copy(12 + i, c, 0, {'k': other}, RING).wait_send()
+
+    load_right.wait()
+    env_before(0)
     h_buf[1] = jnp.zeros(h_buf.shape[1:], jnp.float32)
     v_buf[...] = jnp.zeros(v_buf.shape, jnp.float32)
 
@@ -339,6 +404,7 @@
         same = jnp.broadcast_to(same_ref[...][None], (n_out // 8, 8, n_in)).reshape(n_out, n_in)
         w_mat[...] = wide * same
 
+    env_before(1)
     with scope('gather_early'):
         for message in MESSAGES[:EARLY]:
             take(message, groups)
@@ -367,61 +433,6 @@
                             event()
 
         run(steps)
-
-    up, down, far = y_at[1], y_at[3], y_at[2]
-    strip = right_full.shape[-1] // ENV_PIECES
-
-    def env_copy(kind, c, block, device, count=1, core=None):
-        span = pl.ds(c * strip, strip)
-        row = k if core is None else core
-        view = right_full.at[:, pl.ds(block, count), pl.ds(row, 1), :, span]
-        return pltpu.make_async_remote_copy(
-            src_ref=view, dst_ref=view, send_sem=env_send.at[kind, c], recv_sem=env_recv.at[kind, c],
-            device_id=device, device_id_type=MESH_IDS)
-
-    def block_of(owner, d):
-        return owner * RING + x_at[d]
-
-    TAKEN = (0, 1)
-
-    def env_start(c):
-        for d in TAKEN:
-            env_copy(d, c, block_of(y, d), {'y': up}).start()
-            env_copy(2 + d, c, block_of(y, d), {'y': down}).start()
-
-    def env_pass_x(c, i, owner):
-        env_copy(6 + i, c, block_of(owner, 0), {'x': x_at[1]}).start()
-        env_copy(9 + i, c, block_of(owner, 1), {'x': x_at[3]}).start()
-
-    def env_pass(c):
-        for d in TAKEN:
-            env_copy(d, c, block_of(down, d), {'y': up}).wait_recv()
-            env_copy(2 + d, c, block_of(up, d), {'y': down}).wait_recv()
-        env_copy(4, c, block_of(down, 0), {'y': up}).start()
-        env_copy(5, c, block_of(up, 1), {'y': down}).start()
-        env_pass_x(c, 0, down)
-        env_pass_x(c, 1, up)
-
-    def env_far(c):
-        env_copy(4, c, block_of(far, 0), {'y': up}).wait_recv()
-        env_copy(5, c, block_of(far, 1), {'y': down}).wait_recv()
-        env_pass_x(c, 2, far)
-
-    def env_share(c):
-        for i, owner in enumerate((down, up, far)):
-            env_copy(6 + i, c, block_of(owner, 3), {'x': x_at[1]}).wait_recv()
-            env_copy(9 + i, c, block_of(owner, 2), {'x': x_at[3]}).wait_recv()
-            env_copy(12 + i, c, owner * RING, {'k': other}, RING).start()
-
-    def env_done(c):
-        for i, owner in enumerate((down, up, far)):
-            env_copy(12 + i, c, owner * RING, {'k': other}, RING, other).wait_recv()
-
-    def env_sent(c):
-        for kind in range(12):
-            env_copy(kind, c, 0, {'k': other}).wait_send()
-        for i in range(3):
-            env_copy(12 + i, c, 0, {'k': other}, RING).wait_send()
 
     def way(s):
         return 1 - 2 * lax.rem(s, 2)
@@ -505,11 +516,8 @@
             at = events.setdefault(at, [])
             at += [functools.partial(take, message, groups) for message in queue[:count]]
             queue = queue[count:]
-            for event in (load_right.wait,) * (n == ENV_STEPS[0]):
-                at.append(functools.partial(in_first, event))
-            for first_step, event in zip(ENV_STEPS, (env_start, env_pass, env_far, env_share, env_done)):
-                if 0 <= n - first_step < ENV_PIECES * ENV_STRIDE and (n - first_step) % ENV_STRIDE == 0:
-                    at.append(functools.partial(in_first, event, (n - first_step) // ENV_STRIDE))
+            for event, steps in zip(env_events, ENV_STEPS):
+                at += [functools.partial(in_first, event, c) for c in range(ENV_PIECES) if steps[c] == n + ENV_LEAD]
             if n in CHUNK_STEPS:
                 first, count = CHUNKS[CHUNK_STEPS.index(n)]
                 at += [sibling_copy(i).wait_recv for i in range(first // GROUP, (first + count) // GROUP)]

time: 465 us -> 457 us (0.983)
  Pallas kernels: 460 us -> 452 us
    pallas_call x1, Pallas kernels: 460 us -> 452 us  [local_run(): pl.pallas_call(functools.partial(lanczos_kernel, float(psi_blk.size * gri...]
where the time goes in v6:
time: 457 us
  Pallas kernels  452 us (99%)
  local copies, waits for them, and re-layouts  5 us (1%)
    pallas_call x1, Pallas kernels, local_run(): pl.pallas_call(functools.partial(lanczos_kernel, float(psi_blk.size * gri...  452 us

profile of v6, /device:TPU:1, one launch (start us, length us, event | category | flops | bytes accessed | tf_op | source)
XLA Modules:
  0.0 457.2 jit_solution(16656956710566939700)
XLA Ops:
  0.6 1.7 reshape.20.mpo_ref
  2.4 451.5 %shard_map.94 = (f32[9,64,256]{2,1,0:T(8,128)}, f32[2,5,8,128]{3,2,1,0:T(8,128)}) custom-call(f32[9,64,256]{2,1,0:T(8,128)} %bitcast.14, f32[5,256,2048]{2,1,0:T(8,128)} %bitcast.11, f32[5,4,2,8,2048]{4,3,2,1,0:T(8,128)} %bitcast.12, f32[45,45]{1,0:T(8,128)} %reshape.20.mpo_ref, f32[360,45]{1,0:T(8,128)} %constant.6.clone.spread_out_ref, ...), custom_call_target="tpu_custom_call" | custom-call | tf_op jit(solution)/shard_map/pallas_call | solution.py:765
  453.9 1.4 slice_reduce_fusion
  455.3 1.9 copy.11

commit v7 on v6

--- a/solution.py
+++ b/solution.py
@@ -20,7 +20,7 @@
 CORES = 2
 PARTS = 4
 STREAMS = 2
-TREES = 4
+TREES = 8
 BLOCKS = RING * RING
 ALL_LINKS = [('x', 1), ('y', 1), ('x', -1), ('y', -1)]
 
@@ -86,16 +86,16 @@
     return [int(c, 36) for text in texts for c in text]
 
 
-RELEASE = [0, 2.9, 4.5, 8.0]
-PAIR_ORDER = counts('0101220013132323')
-LAGS = (counts('11011'), counts('35040'), counts('39276'), counts('17387'))
-FINISH = [9, 17, 23, 24]
-HOOKS = (7, 15, 30)
-DURING_ONE = counts('500020104111105222303030100', '301300')
+RELEASE = [0, 0, 0, 0, 8.0, 8.0, 8.0, 8.0]
+PAIR_ORDER = counts('0101200112332233')
+LAGS = (counts('11023'), counts('14233'), counts('32455'), counts('22255'))
+FINISH = [11, 14, 21, 22]
+HOOKS = (6, 15, 30)
+DURING_ONE = counts('311703122404652560300724111', '542200')
 DURING_RING = counts('0000000000000400')
-DURING_TAIL = counts('000102004010301')
+DURING_TAIL = counts('13500529211120')
 EARLY = sum(DURING_RING) + sum(DURING_TAIL)
-ENV_STEPS = (counts('g515i4mp'), counts('sa2btbvw'), counts('wh8kwrww'), counts('wkbnwtxw'), counts('xontywyx'))
+ENV_STEPS = (counts('7d2ji2op'), counts('hjarnatv'), counts('mpgtqhuw'), counts('nqkurlvw'), counts('qxqwwywy'))
 ENV_PIECES = len(ENV_STEPS[0])
 ENV_LEAD = 2
 CHUNK_STEPS = (0, 9, 18, 27, 30)
@@ -312,8 +312,13 @@
         index = INDEX[message]
         return pltpu.make_async_remote_copy(
             src_ref=gath.at[0, INDEX[source_of(message)]], dst_ref=gath.at[0, index],
-            send_sem=ag_send.at[index], recv_sem=ag_recv.at[index],
+            send_sem=ag_send.at[MESSAGES.index(message)], recv_sem=ag_recv.at[MESSAGES.index(message)],
             device_id=step_to(*LINKS[message]), device_id_type=MESH_IDS)
+
+    def gather_sent(index):
+        pltpu.make_async_remote_copy(
+            src_ref=gath.at[0, index], dst_ref=gath.at[0, index], send_sem=ag_send.at[index], recv_sem=ag_recv.at[index],
+            device_id=step_to(*ALL_LINKS[0]), device_id_type=MESH_IDS).wait_send()
 
     def sibling_copy(index):
         span = pl.ds(index * GROUP, GROUP)
@@ -542,8 +547,7 @@
         repeat(0, wide_steps, wide_step)
         repeat(0, half_steps, half_step)
         with scope('gather_sent'):
-            for message in MESSAGES:
-                gather_copy(message).wait_send()
+            repeat(0, len(MESSAGES), gather_sent)
             repeat(0, BLOCKS, lambda i: sibling_copy(i).wait_send())
 
         @pl.when(more)
@@ -792,8 +796,8 @@
                 pltpu.VMEM((2, 2) + TILE, f32),
                 pltpu.VMEM((2, red) + TILE, f32),
                 pltpu.VMEM(TILE, f32),
-                pltpu.SemaphoreType.DMA((len(HELD),)),
-                pltpu.SemaphoreType.DMA((len(HELD),)),
+                pltpu.SemaphoreType.DMA((len(MESSAGES),)),
+                pltpu.SemaphoreType.DMA((len(MESSAGES),)),
                 pltpu.SemaphoreType.DMA((BLOCKS,)),
                 pltpu.SemaphoreType.DMA((BLOCKS,)),
                 pltpu.SemaphoreType.DMA((PARTS, num_z - 1, STREAMS)),

time: 457 us -> 457 us (level)
  no operation moved by 1% of the time
where the time goes in v7:
time: 457 us
  Pallas kernels  451 us (99%)
  local copies, waits for them, and re-layouts  5 us (1%)
    pallas_call x1, Pallas kernels, local_run(): pl.pallas_call(functools.partial(lanczos_kernel, float(psi_blk.size * gri...  451 us

profile of v7, /device:TPU:1, one launch (start us, length us, event | category | flops | bytes accessed | tf_op | source)
XLA Modules:
  0.0 457.1 jit_solution(5434987429332778938)
XLA Ops:
  0.6 1.7 reshape.20.mpo_ref
  2.4 451.4 %shard_map.94 = (f32[9,64,256]{2,1,0:T(8,128)}, f32[2,5,8,128]{3,2,1,0:T(8,128)}) custom-call(f32[9,64,256]{2,1,0:T(8,128)} %bitcast.14, f32[5,256,2048]{2,1,0:T(8,128)} %bitcast.11, f32[5,4,2,8,2048]{4,3,2,1,0:T(8,128)} %bitcast.12, f32[45,45]{1,0:T(8,128)} %reshape.20.mpo_ref, f32[360,45]{1,0:T(8,128)} %constant.6.clone.spread_out_ref, ...), custom_call_target="tpu_custom_call" | custom-call | tf_op jit(solution)/shard_map/pallas_call | solution.py:769
  453.8 1.4 slice_reduce_fusion
  455.2 1.9 copy.11

commit v8 on v6

--- a/solution.py
+++ b/solution.py
@@ -312,8 +312,13 @@
         index = INDEX[message]
         return pltpu.make_async_remote_copy(
             src_ref=gath.at[0, INDEX[source_of(message)]], dst_ref=gath.at[0, index],
-            send_sem=ag_send.at[index], recv_sem=ag_recv.at[index],
+            send_sem=ag_send.at[MESSAGES.index(message)], recv_sem=ag_recv.at[MESSAGES.index(message)],
             device_id=step_to(*LINKS[message]), device_id_type=MESH_IDS)
+
+    def gather_sent(index):
+        pltpu.make_async_remote_copy(
+            src_ref=gath.at[0, index], dst_ref=gath.at[0, index], send_sem=ag_send.at[index], recv_sem=ag_recv.at[index],
+            device_id=step_to(*ALL_LINKS[0]), device_id_type=MESH_IDS).wait_send()
 
     def sibling_copy(index):
         span = pl.ds(index * GROUP, GROUP)
@@ -344,22 +349,6 @@
     def own_parts(s):
         each = TREES // PARTS
         return [(s * each + i, 0, 0) for i in range(each)]
-
-    with scope('turn_wait'):
-        turn_finish(0)
-    with scope('turn'):
-        def unpack(pair):
-            block = jnp.transpose(turned(0, pair))
-            for i, p in enumerate((2 * pair, jnp.minimum(2 * pair + 1, phys - 1))):
-                h_buf[0, p] = block[i * rows:(i + 1) * rows, :]
-                for part in range(TREES):
-                    span = slice(i * rows + part * piece, i * rows + (part + 1) * piece)
-                    gath[0, INDEX[part, 0, 0], p] = block[span, :]
-        repeat(0, pairs, unpack)
-    own = [message for message in HELD if message not in LINKS]
-    groups = groups_after((), own + MESSAGES[:EARLY])
-    for message in own:
-        take(message, groups)
 
     with scope('left'):
         load_left.wait()
@@ -403,6 +392,22 @@
         n_out, n_in = w_mat.shape
         same = jnp.broadcast_to(same_ref[...][None], (n_out // 8, 8, n_in)).reshape(n_out, n_in)
         w_mat[...] = wide * same
+
+    with scope('turn_wait'):
+        turn_finish(0)
+    with scope('turn'):
+        def unpack(pair):
+            block = jnp.transpose(turned(0, pair))
+            for i, p in enumerate((2 * pair, jnp.minimum(2 * pair + 1, phys - 1))):
+                h_buf[0, p] = block[i * rows:(i + 1) * rows, :]
+                for part in range(TREES):
+                    span = slice(i * rows + part * piece, i * rows + (part + 1) * piece)
+                    gath[0, INDEX[part, 0, 0], p] = block[span, :]
+        repeat(0, pairs, unpack)
+    own = [message for message in HELD if message not in LINKS]
+    groups = groups_after((), own + MESSAGES[:EARLY])
+    for message in own:
+        take(message, groups)
 
     env_before(1)
     with scope('gather_early'):
@@ -542,8 +547,7 @@
         repeat(0, wide_steps, wide_step)
         repeat(0, half_steps, half_step)
         with scope('gather_sent'):
-            for message in MESSAGES:
-                gather_copy(message).wait_send()
+            repeat(0, len(MESSAGES), gather_sent)
             repeat(0, BLOCKS, lambda i: sibling_copy(i).wait_send())
 
         @pl.when(more)
@@ -792,8 +796,8 @@
                 pltpu.VMEM((2, 2) + TILE, f32),
                 pltpu.VMEM((2, red) + TILE, f32),
                 pltpu.VMEM(TILE, f32),
-                pltpu.SemaphoreType.DMA((len(HELD),)),
-                pltpu.SemaphoreType.DMA((len(HELD),)),
+                pltpu.SemaphoreType.DMA((len(MESSAGES),)),
+                pltpu.SemaphoreType.DMA((len(MESSAGES),)),
                 pltpu.SemaphoreType.DMA((BLOCKS,)),
                 pltpu.SemaphoreType.DMA((BLOCKS,)),
                 pltpu.SemaphoreType.DMA((PARTS, num_z - 1, STREAMS)),

time: 457 us -> 458 us (level)
  no operation moved by 1% of the time
where the time goes in v8:
time: 458 us
  Pallas kernels  452 us (99%)
  local copies, waits for them, and re-layouts  5 us (1%)
    pallas_call x1, Pallas kernels, local_run(): pl.pallas_call(functools.partial(lanczos_kernel, float(psi_blk.size * gri...  452 us

profile of v8, /device:TPU:1, one launch (start us, length us, event | category | flops | bytes accessed | tf_op | source)
XLA Modules:
  0.0 457.9 jit_solution(15436950281142092822)
XLA Ops:
  0.6 1.7 reshape.20.mpo_ref
  2.4 452.3 %shard_map.94 = (f32[9,64,256]{2,1,0:T(8,128)}, f32[2,5,8,128]{3,2,1,0:T(8,128)}) custom-call(f32[9,64,256]{2,1,0:T(8,128)} %bitcast.14, f32[5,256,2048]{2,1,0:T(8,128)} %bitcast.11, f32[5,4,2,8,2048]{4,3,2,1,0:T(8,128)} %bitcast.12, f32[45,45]{1,0:T(8,128)} %reshape.20.mpo_ref, f32[360,45]{1,0:T(8,128)} %constant.6.clone.spread_out_ref, ...), custom_call_target="tpu_custom_call" | custom-call | tf_op jit(solution)/shard_map/pallas_call | solution.py:769
  454.7 1.4 slice_reduce_fusion
  456.0 1.9 copy.11
